TPU v7x, 32 devices: a 4x4x1 block of a 4x4x8 slice. The times are simulated.
32 devices in a mesh: dp: 1 (over z), tp: 4 (over y), pp: 8 (over x, core).
Axes of the slice: x: 4, y: 4, z: 1, core: 2. Of those that a mesh axis runs over, the one named last changes fastest.
The devices are a block of a 4x4x8 slice.
Arguments:
- x_in: bfloat16 [16, 8, 128, 1024], P(None, 'dp', 'tp')
- ln_params: float32 [8, 4, 1024], P('pp')
- w_q: bfloat16 [8, 1024, 16, 1, 64], P('pp', None, 'tp')
- w_k: bfloat16 [8, 1024, 16, 64], P('pp', None, 'tp')
- w_v: bfloat16 [8, 1024, 16, 64], P('pp', None, 'tp')
- w_o: bfloat16 [8, 16, 1, 64, 1024], P('pp', 'tp')
- w_up: bfloat16 [8, 1024, 4096], P('pp', None, 'tp')
- w_down: bfloat16 [8, 4096, 1024], P('pp', 'tp')
Outputs:
- output: bfloat16 [8, 16, 8, 128, 1024], P('pp', None, 'dp', 'tp')
All inputs are finite; a program needn't handle non-finite values.
Results may differ from a plain program's by a relative error of at most 0.02.
Values are sent between devices in bfloat16 or wider.
A program may use at most 768 MiB of HBM per device.

v0:
```python
import jax
import jax.numpy as jnp
from jax import lax
from jax.sharding import PartitionSpec as P

LN_EPS = 1e-5
ROPE_BASE = 10000.0


def layer_norm(x_act, ln_gain, ln_bias):
    x_f32 = x_act.astype(jnp.float32)
    row_mean = jnp.mean(x_f32, axis=-1, keepdims=True)
    centred = x_f32 - row_mean
    variance = jnp.mean(centred * centred, axis=-1, keepdims=True)
    return (centred * lax.rsqrt(variance + LN_EPS) * ln_gain + ln_bias).astype(jnp.bfloat16)


def rope_tables(seq_len, head_dim):
    positions = jnp.arange(seq_len, dtype=jnp.float32)
    inv_freq = ROPE_BASE ** (-2.0 * jnp.arange(head_dim // 2, dtype=jnp.float32) / head_dim)
    angles = positions[:, None] * inv_freq[None, :]
    return jnp.cos(angles), jnp.sin(angles)


def apply_rope(proj, cos_tab, sin_tab):
    half_dim = proj.shape[-1] // 2
    table_shape = (1, proj.shape[1]) + (1,) * (proj.ndim - 3) + (half_dim,)
    cos_bcast = cos_tab.reshape(table_shape)
    sin_bcast = sin_tab.reshape(table_shape)
    first_half = proj[..., :half_dim]
    second_half = proj[..., half_dim:]
    return jnp.concatenate([first_half * cos_bcast - second_half * sin_bcast, second_half * cos_bcast + first_half * sin_bcast], axis=-1)


def causal_attention(q_proj, k_proj, v_proj):
    seq_len = q_proj.shape[1]
    scores = jnp.einsum("btkgh,bskh->bktgs", q_proj, k_proj, preferred_element_type=jnp.float32) * (q_proj.shape[-1] ** -0.5)
    positions = jnp.arange(seq_len)
    allowed = positions[:, None, None] >= positions[None, None, :]
    probs_bf = jax.nn.softmax(jnp.where(allowed, scores, -1e30), axis=-1).astype(jnp.bfloat16)
    return jnp.einsum("bktgs,bskh->bktgh", probs_bf, v_proj, preferred_element_type=jnp.float32).astype(jnp.bfloat16)


def branch_partial(x_full, ln_par, w_q, w_k, w_v, w_o, w_up, w_down):
    batch_dim, seq_len, d_model = x_full.shape
    kv_local, group_size, head_dim = w_q.shape[1:]
    num_rows = batch_dim * seq_len
    h_attn = layer_norm(x_full, ln_par[0], ln_par[1]).reshape(num_rows, d_model)
    h_mlp = layer_norm(x_full, ln_par[2], ln_par[3]).reshape(num_rows, d_model)
    cos_tab, sin_tab = rope_tables(seq_len, head_dim)
    q_proj = jnp.dot(h_attn, w_q.reshape(d_model, -1), preferred_element_type=jnp.float32)
    q_proj = apply_rope(q_proj.reshape(batch_dim, seq_len, kv_local, group_size, head_dim), cos_tab, sin_tab).astype(jnp.bfloat16)
    k_proj = jnp.dot(h_attn, w_k.reshape(d_model, -1), preferred_element_type=jnp.float32)
    k_proj = apply_rope(k_proj.reshape(batch_dim, seq_len, kv_local, head_dim), cos_tab, sin_tab).astype(jnp.bfloat16)
    v_proj = jnp.dot(h_attn, w_v.reshape(d_model, -1), preferred_element_type=jnp.float32).astype(jnp.bfloat16)
    v_proj = v_proj.reshape(batch_dim, seq_len, kv_local, head_dim)
    context = causal_attention(q_proj, k_proj, v_proj)
    attn_out = jnp.einsum("bktgh,kghd->btd", context, w_o, preferred_element_type=jnp.float32)
    hidden = jax.nn.gelu(jnp.dot(h_mlp, w_up, preferred_element_type=jnp.float32), approximate=False).astype(jnp.bfloat16)
    mlp_out = jnp.dot(hidden, w_down, preferred_element_type=jnp.float32).reshape(batch_dim, seq_len, d_model)
    return (attn_out + mlp_out).astype(jnp.bfloat16)


def solution(mesh):
    pp_size = mesh.shape["pp"]
    send_pairs = [(src_idx, src_idx + 1) for src_idx in range(pp_size - 1)]

    def stage_layer(x_shard, layer_weights):
        ln_par, wq_s, wk_s, wv_s, wo_s, wup_s, wdown_s = layer_weights
        x_full = lax.all_gather(x_shard, "tp", axis=1, tiled=True)
        partial_sum = branch_partial(x_full, ln_par, wq_s, wk_s, wv_s, wo_s, wup_s, wdown_s)
        reduced = lax.psum_scatter(partial_sum, "tp", scatter_dimension=1, tiled=True)
        return (x_shard.astype(jnp.float32) + reduced.astype(jnp.float32)).astype(jnp.bfloat16)

    def stage_body(x_in, ln_params, w_q, w_k, w_v, w_o, w_up, w_down):
        stage_idx = lax.axis_index("pp")
        num_micro = x_in.shape[0]
        layer_weights = (ln_params[0], w_q[0], w_k[0], w_v[0], w_o[0], w_up[0], w_down[0])

        def micro_step(step_idx, loop_carry):
            recv_buf, out_buf = loop_carry
            first_in = lax.dynamic_index_in_dim(x_in, jnp.minimum(step_idx, num_micro - 1), axis=0, keepdims=False)
            layer_in = jnp.where(stage_idx == 0, first_in, recv_buf)
            layer_out = stage_layer(layer_in, layer_weights)
            slot_idx = step_idx - stage_idx
            is_valid = (slot_idx >= 0) & (slot_idx < num_micro)
            slot_safe = jnp.clip(slot_idx, 0, num_micro - 1)
            previous = lax.dynamic_index_in_dim(out_buf, slot_safe, axis=0, keepdims=False)
            out_buf = lax.dynamic_update_index_in_dim(out_buf, jnp.where(is_valid, layer_out, previous), slot_safe, axis=0)
            recv_buf = lax.ppermute(layer_out, "pp", send_pairs)
            return recv_buf, out_buf

        init_carry = (jnp.zeros_like(x_in[0]), jnp.zeros_like(x_in))
        _, out_buf = lax.fori_loop(0, num_micro + pp_size - 1, micro_step, init_carry)
        return out_buf[None]

    in_specs = (P(None, "dp", "tp", None), P("pp", None, None), P("pp", None, "tp", None, None), P("pp", None, "tp", None), P("pp", None, "tp", None), P("pp", "tp", None, None, None), P("pp", None, "tp"), P("pp", "tp", None))
    return jax.shard_map(stage_body, mesh=mesh, in_specs=in_specs, out_specs=P("pp", None, "dp", "tp", None), check_vma=False)
```

profile of v0, /device:TPU:103, one launch (start us, length us, event | category | flops | bytes accessed | tf_op | source)
XLA Modules:
  0.0 2519.5 jit_solution(17741115770830827482)
XLA Ops:
  11.1 2501.8 %while.17 = (s32[]{:T(128)}, bf16[8,32,1024]{2,1,0:T(8,128)(2,1)S(1)}, bf16[16,8,32,1024]{3,2,1,0:T(8,128)(2,1)}, pred[]{:T(512)}, bf16[16,8,32,1024]{3,2,1,0:T(...) while((s32[]{:T(128)}, ...), condition=%wide.region_6.7_spmd, body=%wide.region_0.6_spmd.sunk | while | flops 6672110592 | bytes 86233872 | solution.py:94
  13.4 30.5 %all-gather.2.cloned.1.call-done = bf16[8,128,1024]{2,1,0:T(8,128)(2,1)} async-done(((bf16[8,32,1024]{2,1,0:T(8,128)(2,1)}), bf16[8,128,1024]{2,1,0:T(8,128)(2,1)}) %all-gather.2.cloned.1.call-update) | async-done | bytes 2097168 | tf_op jit(solution)/shard_map/while/body/eval_jaxpr/all_gather | solution.py:70
  58.2 17.2 fusion.151
  84.0 26.2 %reduce-scatter.2.cloned.1.call-done = bf16[8,32,1024]{2,1,0:T(8,128)(2,1)} async-done(((bf16[8,128,1024]{2,1,0:T(8,128)(2,1)}), bf16[8,32,1024]{2,1,0:T(8,128)(2,1)}) %reduce-scatter.2.cloned.1.call-update) | async-done | bytes 524304 | tf_op jit(solution)/shard_map/while/body/eval_jaxpr/reduce_scatter | solution.py:72
  118.9 34.1 %all-gather.2.cloned.1.call-done = bf16[8,128,1024]{2,1,0:T(8,128)(2,1)} async-done(((bf16[8,32,1024]{2,1,0:T(8,128)(2,1)}), bf16[8,128,1024]{2,1,0:T(8,128)(2,1)}) %all-gather.2.cloned.1.call-update) | async-done | bytes 2097168 | tf_op jit(solution)/shard_map/while/body/eval_jaxpr/all_gather | solution.py:70
  167.2 17.2 fusion.151
  193.0 26.2 %reduce-scatter.2.cloned.1.call-done = bf16[8,32,1024]{2,1,0:T(8,128)(2,1)} async-done(((bf16[8,128,1024]{2,1,0:T(8,128)(2,1)}), bf16[8,32,1024]{2,1,0:T(8,128)(2,1)}) %reduce-scatter.2.cloned.1.call-update) | async-done | bytes 524304 | tf_op jit(solution)/shard_map/while/body/eval_jaxpr/reduce_scatter | solution.py:72
  227.9 33.9 %all-gather.2.cloned.1.call-done = bf16[8,128,1024]{2,1,0:T(8,128)(2,1)} async-done(((bf16[8,32,1024]{2,1,0:T(8,128)(2,1)}), bf16[8,128,1024]{2,1,0:T(8,128)(2,1)}) %all-gather.2.cloned.1.call-update) | async-done | bytes 2097168 | tf_op jit(solution)/shard_map/while/body/eval_jaxpr/all_gather | solution.py:70
  276.0 17.2 fusion.151
  301.8 26.2 %reduce-scatter.2.cloned.1.call-done = bf16[8,32,1024]{2,1,0:T(8,128)(2,1)} async-done(((bf16[8,128,1024]{2,1,0:T(8,128)(2,1)}), bf16[8,32,1024]{2,1,0:T(8,128)(2,1)}) %reduce-scatter.2.cloned.1.call-update) | async-done | bytes 524304 | tf_op jit(solution)/shard_map/while/body/eval_jaxpr/reduce_scatter | solution.py:72
  336.7 34.1 %all-gather.2.cloned.1.call-done = bf16[8,128,1024]{2,1,0:T(8,128)(2,1)} async-done(((bf16[8,32,1024]{2,1,0:T(8,128)(2,1)}), bf16[8,128,1024]{2,1,0:T(8,128)(2,1)}) %all-gather.2.cloned.1.call-update) | async-done | bytes 2097168 | tf_op jit(solution)/shard_map/while/body/eval_jaxpr/all_gather | solution.py:70
  385.1 17.1 fusion.151
  410.9 26.2 %reduce-scatter.2.cloned.1.call-done = bf16[8,32,1024]{2,1,0:T(8,128)(2,1)} async-done(((bf16[8,128,1024]{2,1,0:T(8,128)(2,1)}), bf16[8,32,1024]{2,1,0:T(8,128)(2,1)}) %reduce-scatter.2.cloned.1.call-update) | async-done | bytes 524304 | tf_op jit(solution)/shard_map/while/body/eval_jaxpr/reduce_scatter | solution.py:72
  445.7 34.1 %all-gather.2.cloned.1.call-done = bf16[8,128,1024]{2,1,0:T(8,128)(2,1)} async-done(((bf16[8,32,1024]{2,1,0:T(8,128)(2,1)}), bf16[8,128,1024]{2,1,0:T(8,128)(2,1)}) %all-gather.2.cloned.1.call-update) | async-done | bytes 2097168 | tf_op jit(solution)/shard_map/while/body/eval_jaxpr/all_gather | solution.py:70
  494.1 17.1 fusion.151
  519.9 26.2 %reduce-scatter.2.cloned.1.call-done = bf16[8,32,1024]{2,1,0:T(8,128)(2,1)} async-done(((bf16[8,128,1024]{2,1,0:T(8,128)(2,1)}), bf16[8,32,1024]{2,1,0:T(8,128)(2,1)}) %reduce-scatter.2.cloned.1.call-update) | async-done | bytes 524304 | tf_op jit(solution)/shard_map/while/body/eval_jaxpr/reduce_scatter | solution.py:72
  554.8 34.1 %all-gather.2.cloned.1.call-done = bf16[8,128,1024]{2,1,0:T(8,128)(2,1)} async-done(((bf16[8,32,1024]{2,1,0:T(8,128)(2,1)}), bf16[8,128,1024]{2,1,0:T(8,128)(2,1)}) %all-gather.2.cloned.1.call-update) | async-done | bytes 2097168 | tf_op jit(solution)/shard_map/while/body/eval_jaxpr/all_gather | solution.py:70
  603.1 17.1 fusion.151
  628.9 26.2 %reduce-scatter.2.cloned.1.call-done = bf16[8,32,1024]{2,1,0:T(8,128)(2,1)} async-done(((bf16[8,128,1024]{2,1,0:T(8,128)(2,1)}), bf16[8,32,1024]{2,1,0:T(8,128)(2,1)}) %reduce-scatter.2.cloned.1.call-update) | async-done | bytes 524304 | tf_op jit(solution)/shard_map/while/body/eval_jaxpr/reduce_scatter | solution.py:72
  663.8 34.1 %all-gather.2.cloned.1.call-done = bf16[8,128,1024]{2,1,0:T(8,128)(2,1)} async-done(((bf16[8,32,1024]{2,1,0:T(8,128)(2,1)}), bf16[8,128,1024]{2,1,0:T(8,128)(2,1)}) %all-gather.2.cloned.1.call-update) | async-done | bytes 2097168 | tf_op jit(solution)/shard_map/while/body/eval_jaxpr/all_gather | solution.py:70
  712.1 17.1 fusion.151
  737.9 26.2 %reduce-scatter.2.cloned.1.call-done = bf16[8,32,1024]{2,1,0:T(8,128)(2,1)} async-done(((bf16[8,128,1024]{2,1,0:T(8,128)(2,1)}), bf16[8,32,1024]{2,1,0:T(8,128)(2,1)}) %reduce-scatter.2.cloned.1.call-update) | async-done | bytes 524304 | tf_op jit(solution)/shard_map/while/body/eval_jaxpr/reduce_scatter | solution.py:72
  772.8 33.9 %all-gather.2.cloned.1.call-done = bf16[8,128,1024]{2,1,0:T(8,128)(2,1)} async-done(((bf16[8,32,1024]{2,1,0:T(8,128)(2,1)}), bf16[8,128,1024]{2,1,0:T(8,128)(2,1)}) %all-gather.2.cloned.1.call-update) | async-done | bytes 2097168 | tf_op jit(solution)/shard_map/while/body/eval_jaxpr/all_gather | solution.py:70
  820.9 17.1 fusion.151
  846.7 26.2 %reduce-scatter.2.cloned.1.call-done = bf16[8,32,1024]{2,1,0:T(8,128)(2,1)} async-done(((bf16[8,128,1024]{2,1,0:T(8,128)(2,1)}), bf16[8,32,1024]{2,1,0:T(8,128)(2,1)}) %reduce-scatter.2.cloned.1.call-update) | async-done | bytes 524304 | tf_op jit(solution)/shard_map/while/body/eval_jaxpr/reduce_scatter | solution.py:72
  881.6 33.9 %all-gather.2.cloned.1.call-done = bf16[8,128,1024]{2,1,0:T(8,128)(2,1)} async-done(((bf16[8,32,1024]{2,1,0:T(8,128)(2,1)}), bf16[8,128,1024]{2,1,0:T(8,128)(2,1)}) %all-gather.2.cloned.1.call-update) | async-done | bytes 2097168 | tf_op jit(solution)/shard_map/while/body/eval_jaxpr/all_gather | solution.py:70
  929.7 17.1 fusion.151
  955.5 26.2 %reduce-scatter.2.cloned.1.call-done = bf16[8,32,1024]{2,1,0:T(8,128)(2,1)} async-done(((bf16[8,128,1024]{2,1,0:T(8,128)(2,1)}), bf16[8,32,1024]{2,1,0:T(8,128)(2,1)}) %reduce-scatter.2.cloned.1.call-update) | async-done | bytes 524304 | tf_op jit(solution)/shard_map/while/body/eval_jaxpr/reduce_scatter | solution.py:72
  990.3 34.1 %all-gather.2.cloned.1.call-done = bf16[8,128,1024]{2,1,0:T(8,128)(2,1)} async-done(((bf16[8,32,1024]{2,1,0:T(8,128)(2,1)}), bf16[8,128,1024]{2,1,0:T(8,128)(2,1)}) %all-gather.2.cloned.1.call-update) | async-done | bytes 2097168 | tf_op jit(solution)/shard_map/while/body/eval_jaxpr/all_gather | solution.py:70
  1038.7 17.1 fusion.151
  1064.5 26.2 %reduce-scatter.2.cloned.1.call-done = bf16[8,32,1024]{2,1,0:T(8,128)(2,1)} async-done(((bf16[8,128,1024]{2,1,0:T(8,128)(2,1)}), bf16[8,32,1024]{2,1,0:T(8,128)(2,1)}) %reduce-scatter.2.cloned.1.call-update) | async-done | bytes 524304 | tf_op jit(solution)/shard_map/while/body/eval_jaxpr/reduce_scatter | solution.py:72
  1099.4 34.1 %all-gather.2.cloned.1.call-done = bf16[8,128,1024]{2,1,0:T(8,128)(2,1)} async-done(((bf16[8,32,1024]{2,1,0:T(8,128)(2,1)}), bf16[8,128,1024]{2,1,0:T(8,128)(2,1)}) %all-gather.2.cloned.1.call-update) | async-done | bytes 2097168 | tf_op jit(solution)/shard_map/while/body/eval_jaxpr/all_gather | solution.py:70
  1173.5 26.2 %reduce-scatter.2.cloned.1.call-done = bf16[8,32,1024]{2,1,0:T(8,128)(2,1)} async-done(((bf16[8,128,1024]{2,1,0:T(8,128)(2,1)}), bf16[8,32,1024]{2,1,0:T(8,128)(2,1)}) %reduce-scatter.2.cloned.1.call-update) | async-done | bytes 524304 | tf_op jit(solution)/shard_map/while/body/eval_jaxpr/reduce_scatter | solution.py:72
  1208.4 34.1 %all-gather.2.cloned.1.call-done = bf16[8,128,1024]{2,1,0:T(8,128)(2,1)} async-done(((bf16[8,32,1024]{2,1,0:T(8,128)(2,1)}), bf16[8,128,1024]{2,1,0:T(8,128)(2,1)}) %all-gather.2.cloned.1.call-update) | async-done | bytes 2097168 | tf_op jit(solution)/shard_map/while/body/eval_jaxpr/all_gather | solution.py:70
  1256.7 17.1 fusion.151
  1282.5 26.2 %reduce-scatter.2.cloned.1.call-done = bf16[8,32,1024]{2,1,0:T(8,128)(2,1)} async-done(((bf16[8,128,1024]{2,1,0:T(8,128)(2,1)}), bf16[8,32,1024]{2,1,0:T(8,128)(2,1)}) %reduce-scatter.2.cloned.1.call-update) | async-done | bytes 524304 | tf_op jit(solution)/shard_map/while/body/eval_jaxpr/reduce_scatter | solution.py:72
  1317.4 34.1 %all-gather.2.cloned.1.call-done = bf16[8,128,1024]{2,1,0:T(8,128)(2,1)} async-done(((bf16[8,32,1024]{2,1,0:T(8,128)(2,1)}), bf16[8,128,1024]{2,1,0:T(8,128)(2,1)}) %all-gather.2.cloned.1.call-update) | async-done | bytes 2097168 | tf_op jit(solution)/shard_map/while/body/eval_jaxpr/all_gather | solution.py:70
  1391.6 26.2 %reduce-scatter.2.cloned.1.call-done = bf16[8,32,1024]{2,1,0:T(8,128)(2,1)} async-done(((bf16[8,128,1024]{2,1,0:T(8,128)(2,1)}), bf16[8,32,1024]{2,1,0:T(8,128)(2,1)}) %reduce-scatter.2.cloned.1.call-update) | async-done | bytes 524304 | tf_op jit(solution)/shard_map/while/body/eval_jaxpr/reduce_scatter | solution.py:72
  1426.4 33.9 %all-gather.2.cloned.1.call-done = bf16[8,128,1024]{2,1,0:T(8,128)(2,1)} async-done(((bf16[8,32,1024]{2,1,0:T(8,128)(2,1)}), bf16[8,128,1024]{2,1,0:T(8,128)(2,1)}) %all-gather.2.cloned.1.call-update) | async-done | bytes 2097168 | tf_op jit(solution)/shard_map/while/body/eval_jaxpr/all_gather | solution.py:70
  1474.5 17.1 fusion.151
  1500.3 26.2 %reduce-scatter.2.cloned.1.call-done = bf16[8,32,1024]{2,1,0:T(8,128)(2,1)} async-done(((bf16[8,128,1024]{2,1,0:T(8,128)(2,1)}), bf16[8,32,1024]{2,1,0:T(8,128)(2,1)}) %reduce-scatter.2.cloned.1.call-update) | async-done | bytes 524304 | tf_op jit(solution)/shard_map/while/body/eval_jaxpr/reduce_scatter | solution.py:72
  1535.2 34.1 %all-gather.2.cloned.1.call-done = bf16[8,128,1024]{2,1,0:T(8,128)(2,1)} async-done(((bf16[8,32,1024]{2,1,0:T(8,128)(2,1)}), bf16[8,128,1024]{2,1,0:T(8,128)(2,1)}) %all-gather.2.cloned.1.call-update) | async-done | bytes 2097168 | tf_op jit(solution)/shard_map/while/body/eval_jaxpr/all_gather | solution.py:70
  1609.4 26.2 %reduce-scatter.2.cloned.1.call-done = bf16[8,32,1024]{2,1,0:T(8,128)(2,1)} async-done(((bf16[8,128,1024]{2,1,0:T(8,128)(2,1)}), bf16[8,32,1024]{2,1,0:T(8,128)(2,1)}) %reduce-scatter.2.cloned.1.call-update) | async-done | bytes 524304 | tf_op jit(solution)/shard_map/while/body/eval_jaxpr/reduce_scatter | solution.py:72
  1644.2 34.1 %all-gather.2.cloned.1.call-done = bf16[8,128,1024]{2,1,0:T(8,128)(2,1)} async-done(((bf16[8,32,1024]{2,1,0:T(8,128)(2,1)}), bf16[8,128,1024]{2,1,0:T(8,128)(2,1)}) %all-gather.2.cloned.1.call-update) | async-done | bytes 2097168 | tf_op jit(solution)/shard_map/while/body/eval_jaxpr/all_gather | solution.py:70
  1692.6 17.1 fusion.151
  1718.4 26.2 %reduce-scatter.2.cloned.1.call-done = bf16[8,32,1024]{2,1,0:T(8,128)(2,1)} async-done(((bf16[8,128,1024]{2,1,0:T(8,128)(2,1)}), bf16[8,32,1024]{2,1,0:T(8,128)(2,1)}) %reduce-scatter.2.cloned.1.call-update) | async-done | bytes 524304 | tf_op jit(solution)/shard_map/while/body/eval_jaxpr/reduce_scatter | solution.py:72
  1753.3 33.9 %all-gather.2.cloned.1.call-done = bf16[8,128,1024]{2,1,0:T(8,128)(2,1)} async-done(((bf16[8,32,1024]{2,1,0:T(8,128)(2,1)}), bf16[8,128,1024]{2,1,0:T(8,128)(2,1)}) %all-gather.2.cloned.1.call-update) | async-done | bytes 2097168 | tf_op jit(solution)/shard_map/while/body/eval_jaxpr/all_gather | solution.py:70
  1801.4 17.1 fusion.151
  1827.2 26.2 %reduce-scatter.2.cloned.1.call-done = bf16[8,32,1024]{2,1,0:T(8,128)(2,1)} async-done(((bf16[8,128,1024]{2,1,0:T(8,128)(2,1)}), bf16[8,32,1024]{2,1,0:T(8,128)(2,1)}) %reduce-scatter.2.cloned.1.call-update) | async-done | bytes 524304 | tf_op jit(solution)/shard_map/while/body/eval_jaxpr/reduce_scatter | solution.py:72
  1862.0 34.1 %all-gather.2.cloned.1.call-done = bf16[8,128,1024]{2,1,0:T(8,128)(2,1)} async-done(((bf16[8,32,1024]{2,1,0:T(8,128)(2,1)}), bf16[8,128,1024]{2,1,0:T(8,128)(2,1)}) %all-gather.2.cloned.1.call-update) | async-done | bytes 2097168 | tf_op jit(solution)/shard_map/while/body/eval_jaxpr/all_gather | solution.py:70
  1910.4 17.1 fusion.151
  1936.2 26.2 %reduce-scatter.2.cloned.1.call-done = bf16[8,32,1024]{2,1,0:T(8,128)(2,1)} async-done(((bf16[8,128,1024]{2,1,0:T(8,128)(2,1)}), bf16[8,32,1024]{2,1,0:T(8,128)(2,1)}) %reduce-scatter.2.cloned.1.call-update) | async-done | bytes 524304 | tf_op jit(solution)/shard_map/while/body/eval_jaxpr/reduce_scatter | solution.py:72
  1971.1 33.9 %all-gather.2.cloned.1.call-done = bf16[8,128,1024]{2,1,0:T(8,128)(2,1)} async-done(((bf16[8,32,1024]{2,1,0:T(8,128)(2,1)}), bf16[8,128,1024]{2,1,0:T(8,128)(2,1)}) %all-gather.2.cloned.1.call-update) | async-done | bytes 2097168 | tf_op jit(solution)/shard_map/while/body/eval_jaxpr/all_gather | solution.py:70
  2019.2 17.1 fusion.151
  2045.0 26.2 %reduce-scatter.2.cloned.1.call-done = bf16[8,32,1024]{2,1,0:T(8,128)(2,1)} async-done(((bf16[8,128,1024]{2,1,0:T(8,128)(2,1)}), bf16[8,32,1024]{2,1,0:T(8,128)(2,1)}) %reduce-scatter.2.cloned.1.call-update) | async-done | bytes 524304 | tf_op jit(solution)/shard_map/while/body/eval_jaxpr/reduce_scatter | solution.py:72
  2079.8 33.9 %all-gather.2.cloned.1.call-done = bf16[8,128,1024]{2,1,0:T(8,128)(2,1)} async-done(((bf16[8,32,1024]{2,1,0:T(8,128)(2,1)}), bf16[8,128,1024]{2,1,0:T(8,128)(2,1)}) %all-gather.2.cloned.1.call-update) | async-done | bytes 2097168 | tf_op jit(solution)/shard_map/while/body/eval_jaxpr/all_gather | solution.py:70
  2127.9 17.1 fusion.151
  2153.7 26.2 %reduce-scatter.2.cloned.1.call-done = bf16[8,32,1024]{2,1,0:T(8,128)(2,1)} async-done(((bf16[8,128,1024]{2,1,0:T(8,128)(2,1)}), bf16[8,32,1024]{2,1,0:T(8,128)(2,1)}) %reduce-scatter.2.cloned.1.call-update) | async-done | bytes 524304 | tf_op jit(solution)/shard_map/while/body/eval_jaxpr/reduce_scatter | solution.py:72
  2188.6 34.1 %all-gather.2.cloned.1.call-done = bf16[8,128,1024]{2,1,0:T(8,128)(2,1)} async-done(((bf16[8,32,1024]{2,1,0:T(8,128)(2,1)}), bf16[8,128,1024]{2,1,0:T(8,128)(2,1)}) %all-gather.2.cloned.1.call-update) | async-done | bytes 2097168 | tf_op jit(solution)/shard_map/while/body/eval_jaxpr/all_gather | solution.py:70
  2262.8 26.2 %reduce-scatter.2.cloned.1.call-done = bf16[8,32,1024]{2,1,0:T(8,128)(2,1)} async-done(((bf16[8,128,1024]{2,1,0:T(8,128)(2,1)}), bf16[8,32,1024]{2,1,0:T(8,128)(2,1)}) %reduce-scatter.2.cloned.1.call-update) | async-done | bytes 524304 | tf_op jit(solution)/shard_map/while/body/eval_jaxpr/reduce_scatter | solution.py:72
  2297.6 33.9 %all-gather.2.cloned.1.call-done = bf16[8,128,1024]{2,1,0:T(8,128)(2,1)} async-done(((bf16[8,32,1024]{2,1,0:T(8,128)(2,1)}), bf16[8,128,1024]{2,1,0:T(8,128)(2,1)}) %all-gather.2.cloned.1.call-update) | async-done | bytes 2097168 | tf_op jit(solution)/shard_map/while/body/eval_jaxpr/all_gather | solution.py:70
  2371.5 26.2 %reduce-scatter.2.cloned.1.call-done = bf16[8,32,1024]{2,1,0:T(8,128)(2,1)} async-done(((bf16[8,128,1024]{2,1,0:T(8,128)(2,1)}), bf16[8,32,1024]{2,1,0:T(8,128)(2,1)}) %reduce-scatter.2.cloned.1.call-update) | async-done | bytes 524304 | tf_op jit(solution)/shard_map/while/body/eval_jaxpr/reduce_scatter | solution.py:72
  2406.4 33.9 %all-gather.2.cloned.1.call-done = bf16[8,128,1024]{2,1,0:T(8,128)(2,1)} async-done(((bf16[8,32,1024]{2,1,0:T(8,128)(2,1)}), bf16[8,128,1024]{2,1,0:T(8,128)(2,1)}) %all-gather.2.cloned.1.call-update) | async-done | bytes 2097168 | tf_op jit(solution)/shard_map/while/body/eval_jaxpr/all_gather | solution.py:70
  2480.3 26.2 %reduce-scatter.2.cloned.1.call-done = bf16[8,32,1024]{2,1,0:T(8,128)(2,1)} async-done(((bf16[8,128,1024]{2,1,0:T(8,128)(2,1)}), bf16[8,32,1024]{2,1,0:T(8,128)(2,1)}) %reduce-scatter.2.cloned.1.call-update) | async-done | bytes 524304 | tf_op jit(solution)/shard_map/while/body/eval_jaxpr/reduce_scatter | solution.py:72
  (794 shorter events, 830.9 us)
Async XLA Ops:
  11.1 32.8 %all-gather.2.cloned.1.call-start = ((), (), s32[]{:S(2)}) async-start(), calls=%async_computation.1 | async-start | bytes 2621440 | tf_op jit(solution)/shard_map/while/body/eval_jaxpr/all_gather | solution.py:70
  13.1 97.1 %reduce-scatter.2.cloned.1.call-start = ((), (), s32[]{:S(2)}) async-start(), calls=%async_computation.2 | async-start | bytes 2621440 | tf_op jit(solution)/shard_map/while/body/eval_jaxpr/reduce_scatter | solution.py:72
  116.6 36.4 %all-gather.2.cloned.1.call-start = ((), (), s32[]{:S(2)}) async-start(), calls=%async_computation.1 | async-start | bytes 2621440 | tf_op jit(solution)/shard_map/while/body/eval_jaxpr/all_gather | solution.py:70
  118.6 100.6 %reduce-scatter.2.cloned.1.call-start = ((), (), s32[]{:S(2)}) async-start(), calls=%async_computation.2 | async-start | bytes 2621440 | tf_op jit(solution)/shard_map/while/body/eval_jaxpr/reduce_scatter | solution.py:72
  221.4 4.3 collective-permute-start
  225.6 36.1 %all-gather.2.cloned.1.call-start = ((), (), s32[]{:S(2)}) async-start(), calls=%async_computation.1 | async-start | bytes 2621440 | tf_op jit(solution)/shard_map/while/body/eval_jaxpr/all_gather | solution.py:70
  227.6 100.4 %reduce-scatter.2.cloned.1.call-start = ((), (), s32[]{:S(2)}) async-start(), calls=%async_computation.2 | async-start | bytes 2621440 | tf_op jit(solution)/shard_map/while/body/eval_jaxpr/reduce_scatter | solution.py:72
  330.2 4.3 collective-permute-start
  334.4 36.4 %all-gather.2.cloned.1.call-start = ((), (), s32[]{:S(2)}) async-start(), calls=%async_computation.1 | async-start | bytes 2621440 | tf_op jit(solution)/shard_map/while/body/eval_jaxpr/all_gather | solution.py:70
  336.4 100.6 %reduce-scatter.2.cloned.1.call-start = ((), (), s32[]{:S(2)}) async-start(), calls=%async_computation.2 | async-start | bytes 2621440 | tf_op jit(solution)/shard_map/while/body/eval_jaxpr/reduce_scatter | solution.py:72
  439.2 4.3 collective-permute-start
  443.5 36.4 %all-gather.2.cloned.1.call-start = ((), (), s32[]{:S(2)}) async-start(), calls=%async_computation.1 | async-start | bytes 2621440 | tf_op jit(solution)/shard_map/while/body/eval_jaxpr/all_gather | solution.py:70
  445.5 100.6 %reduce-scatter.2.cloned.1.call-start = ((), (), s32[]{:S(2)}) async-start(), calls=%async_computation.2 | async-start | bytes 2621440 | tf_op jit(solution)/shard_map/while/body/eval_jaxpr/reduce_scatter | solution.py:72
  548.2 4.3 collective-permute-start
  552.5 36.4 %all-gather.2.cloned.1.call-start = ((), (), s32[]{:S(2)}) async-start(), calls=%async_computation.1 | async-start | bytes 2621440 | tf_op jit(solution)/shard_map/while/body/eval_jaxpr/all_gather | solution.py:70
  554.5 100.6 %reduce-scatter.2.cloned.1.call-start = ((), (), s32[]{:S(2)}) async-start(), calls=%async_computation.2 | async-start | bytes 2621440 | tf_op jit(solution)/shard_map/while/body/eval_jaxpr/reduce_scatter | solution.py:72
  657.2 4.3 collective-permute-start
  661.5 36.4 %all-gather.2.cloned.1.call-start = ((), (), s32[]{:S(2)}) async-start(), calls=%async_computation.1 | async-start | bytes 2621440 | tf_op jit(solution)/shard_map/while/body/eval_jaxpr/all_gather | solution.py:70
  663.5 100.6 %reduce-scatter.2.cloned.1.call-start = ((), (), s32[]{:S(2)}) async-start(), calls=%async_computation.2 | async-start | bytes 2621440 | tf_op jit(solution)/shard_map/while/body/eval_jaxpr/reduce_scatter | solution.py:72
  766.3 4.3 collective-permute-start
  770.5 36.1 %all-gather.2.cloned.1.call-start = ((), (), s32[]{:S(2)}) async-start(), calls=%async_computation.1 | async-start | bytes 2621440 | tf_op jit(solution)/shard_map/while/body/eval_jaxpr/all_gather | solution.py:70
  772.5 100.3 %reduce-scatter.2.cloned.1.call-start = ((), (), s32[]{:S(2)}) async-start(), calls=%async_computation.2 | async-start | bytes 2621440 | tf_op jit(solution)/shard_map/while/body/eval_jaxpr/reduce_scatter | solution.py:72
  875.0 4.3 collective-permute-start
  879.3 36.1 %all-gather.2.cloned.1.call-start = ((), (), s32[]{:S(2)}) async-start(), calls=%async_computation.1 | async-start | bytes 2621440 | tf_op jit(solution)/shard_map/while/body/eval_jaxpr/all_gather | solution.py:70
  881.3 100.4 %reduce-scatter.2.cloned.1.call-start = ((), (), s32[]{:S(2)}) async-start(), calls=%async_computation.2 | async-start | bytes 2621440 | tf_op jit(solution)/shard_map/while/body/eval_jaxpr/reduce_scatter | solution.py:72
  983.8 4.3 collective-permute-start
  988.1 36.4 %all-gather.2.cloned.1.call-start = ((), (), s32[]{:S(2)}) async-start(), calls=%async_computation.1 | async-start | bytes 2621440 | tf_op jit(solution)/shard_map/while/body/eval_jaxpr/all_gather | solution.py:70
  990.1 100.6 %reduce-scatter.2.cloned.1.call-start = ((), (), s32[]{:S(2)}) async-start(), calls=%async_computation.2 | async-start | bytes 2621440 | tf_op jit(solution)/shard_map/while/body/eval_jaxpr/reduce_scatter | solution.py:72
  1092.8 4.3 collective-permute-start
  1097.1 36.4 %all-gather.2.cloned.1.call-start = ((), (), s32[]{:S(2)}) async-start(), calls=%async_computation.1 | async-start | bytes 2621440 | tf_op jit(solution)/shard_map/while/body/eval_jaxpr/all_gather | solution.py:70
  1099.1 100.6 %reduce-scatter.2.cloned.1.call-start = ((), (), s32[]{:S(2)}) async-start(), calls=%async_computation.2 | async-start | bytes 2621440 | tf_op jit(solution)/shard_map/while/body/eval_jaxpr/reduce_scatter | solution.py:72
  1201.9 4.3 collective-permute-start
  1206.1 36.4 %all-gather.2.cloned.1.call-start = ((), (), s32[]{:S(2)}) async-start(), calls=%async_computation.1 | async-start | bytes 2621440 | tf_op jit(solution)/shard_map/while/body/eval_jaxpr/all_gather | solution.py:70
  1208.1 100.6 %reduce-scatter.2.cloned.1.call-start = ((), (), s32[]{:S(2)}) async-start(), calls=%async_computation.2 | async-start | bytes 2621440 | tf_op jit(solution)/shard_map/while/body/eval_jaxpr/reduce_scatter | solution.py:72
  1310.9 4.3 collective-permute-start
  1315.1 36.4 %all-gather.2.cloned.1.call-start = ((), (), s32[]{:S(2)}) async-start(), calls=%async_computation.1 | async-start | bytes 2621440 | tf_op jit(solution)/shard_map/while/body/eval_jaxpr/all_gather | solution.py:70
  1317.1 100.6 %reduce-scatter.2.cloned.1.call-start = ((), (), s32[]{:S(2)}) async-start(), calls=%async_computation.2 | async-start | bytes 2621440 | tf_op jit(solution)/shard_map/while/body/eval_jaxpr/reduce_scatter | solution.py:72
  1419.9 4.3 collective-permute-start
  1424.2 36.1 %all-gather.2.cloned.1.call-start = ((), (), s32[]{:S(2)}) async-start(), calls=%async_computation.1 | async-start | bytes 2621440 | tf_op jit(solution)/shard_map/while/body/eval_jaxpr/all_gather | solution.py:70
  1426.2 100.3 %reduce-scatter.2.cloned.1.call-start = ((), (), s32[]{:S(2)}) async-start(), calls=%async_computation.2 | async-start | bytes 2621440 | tf_op jit(solution)/shard_map/while/body/eval_jaxpr/reduce_scatter | solution.py:72
  1528.7 4.3 collective-permute-start
  1532.9 36.4 %all-gather.2.cloned.1.call-start = ((), (), s32[]{:S(2)}) async-start(), calls=%async_computation.1 | async-start | bytes 2621440 | tf_op jit(solution)/shard_map/while/body/eval_jaxpr/all_gather | solution.py:70
  1534.9 100.6 %reduce-scatter.2.cloned.1.call-start = ((), (), s32[]{:S(2)}) async-start(), calls=%async_computation.2 | async-start | bytes 2621440 | tf_op jit(solution)/shard_map/while/body/eval_jaxpr/reduce_scatter | solution.py:72
  1637.7 4.3 collective-permute-start
  1642.0 36.4 %all-gather.2.cloned.1.call-start = ((), (), s32[]{:S(2)}) async-start(), calls=%async_computation.1 | async-start | bytes 2621440 | tf_op jit(solution)/shard_map/while/body/eval_jaxpr/all_gather | solution.py:70
  1644.0 100.6 %reduce-scatter.2.cloned.1.call-start = ((), (), s32[]{:S(2)}) async-start(), calls=%async_computation.2 | async-start | bytes 2621440 | tf_op jit(solution)/shard_map/while/body/eval_jaxpr/reduce_scatter | solution.py:72
  1746.7 4.3 collective-permute-start
  1751.0 36.1 %all-gather.2.cloned.1.call-start = ((), (), s32[]{:S(2)}) async-start(), calls=%async_computation.1 | async-start | bytes 2621440 | tf_op jit(solution)/shard_map/while/body/eval_jaxpr/all_gather | solution.py:70
  1753.0 100.4 %reduce-scatter.2.cloned.1.call-start = ((), (), s32[]{:S(2)}) async-start(), calls=%async_computation.2 | async-start | bytes 2621440 | tf_op jit(solution)/shard_map/while/body/eval_jaxpr/reduce_scatter | solution.py:72
  1855.5 4.3 collective-permute-start
  1859.8 36.4 %all-gather.2.cloned.1.call-start = ((), (), s32[]{:S(2)}) async-start(), calls=%async_computation.1 | async-start | bytes 2621440 | tf_op jit(solution)/shard_map/while/body/eval_jaxpr/all_gather | solution.py:70
  1861.8 100.6 %reduce-scatter.2.cloned.1.call-start = ((), (), s32[]{:S(2)}) async-start(), calls=%async_computation.2 | async-start | bytes 2621440 | tf_op jit(solution)/shard_map/while/body/eval_jaxpr/reduce_scatter | solution.py:72
  1964.5 4.3 collective-permute-start
  1968.8 36.1 %all-gather.2.cloned.1.call-start = ((), (), s32[]{:S(2)}) async-start(), calls=%async_computation.1 | async-start | bytes 2621440 | tf_op jit(solution)/shard_map/while/body/eval_jaxpr/all_gather | solution.py:70
  1970.8 100.3 %reduce-scatter.2.cloned.1.call-start = ((), (), s32[]{:S(2)}) async-start(), calls=%async_computation.2 | async-start | bytes 2621440 | tf_op jit(solution)/shard_map/while/body/eval_jaxpr/reduce_scatter | solution.py:72
  2077.6 36.1 %all-gather.2.cloned.1.call-start = ((), (), s32[]{:S(2)}) async-start(), calls=%async_computation.1 | async-start | bytes 2621440 | tf_op jit(solution)/shard_map/while/body/eval_jaxpr/all_gather | solution.py:70
  2079.6 100.4 %reduce-scatter.2.cloned.1.call-start = ((), (), s32[]{:S(2)}) async-start(), calls=%async_computation.2 | async-start | bytes 2621440 | tf_op jit(solution)/shard_map/while/body/eval_jaxpr/reduce_scatter | solution.py:72
  2186.3 36.4 %all-gather.2.cloned.1.call-start = ((), (), s32[]{:S(2)}) async-start(), calls=%async_computation.1 | async-start | bytes 2621440 | tf_op jit(solution)/shard_map/while/body/eval_jaxpr/all_gather | solution.py:70
  2188.3 100.6 %reduce-scatter.2.cloned.1.call-start = ((), (), s32[]{:S(2)}) async-start(), calls=%async_computation.2 | async-start | bytes 2621440 | tf_op jit(solution)/shard_map/while/body/eval_jaxpr/reduce_scatter | solution.py:72
  2291.1 4.3 collective-permute-start
  2295.4 36.1 %all-gather.2.cloned.1.call-start = ((), (), s32[]{:S(2)}) async-start(), calls=%async_computation.1 | async-start | bytes 2621440 | tf_op jit(solution)/shard_map/while/body/eval_jaxpr/all_gather | solution.py:70
  2297.4 100.3 %reduce-scatter.2.cloned.1.call-start = ((), (), s32[]{:S(2)}) async-start(), calls=%async_computation.2 | async-start | bytes 2621440 | tf_op jit(solution)/shard_map/while/body/eval_jaxpr/reduce_scatter | solution.py:72
  2404.1 36.1 %all-gather.2.cloned.1.call-start = ((), (), s32[]{:S(2)}) async-start(), calls=%async_computation.1 | async-start | bytes 2621440 | tf_op jit(solution)/shard_map/while/body/eval_jaxpr/all_gather | solution.py:70
  2406.1 100.4 %reduce-scatter.2.cloned.1.call-start = ((), (), s32[]{:S(2)}) async-start(), calls=%async_computation.2 | async-start | bytes 2621440 | tf_op jit(solution)/shard_map/while/body/eval_jaxpr/reduce_scatter | solution.py:72
  (99 other events, 1710.3 us)
Sparse Core Ops, SparseCore 0:
  13.5 30.4 all-gather.1
  83.0 27.1 reduce-scatter.1
  119.0 33.9 all-gather.1
  192.0 27.1 reduce-scatter.1
  227.8 33.9 all-gather.1
  300.8 27.1 reduce-scatter.1
  336.8 33.9 all-gather.1
  409.8 27.1 reduce-scatter.1
  445.8 33.9 all-gather.1
  518.9 27.1 reduce-scatter.1
  554.8 33.9 all-gather.1
  627.9 27.1 reduce-scatter.1
  663.9 33.9 all-gather.1
  736.9 27.1 reduce-scatter.1
  772.6 33.9 all-gather.1
  845.7 27.1 reduce-scatter.1
  881.4 33.9 all-gather.1
  954.5 27.1 reduce-scatter.1
  990.4 33.9 all-gather.1
  1063.5 27.1 reduce-scatter.1
  1099.5 33.9 all-gather.1
  1172.5 27.1 reduce-scatter.1
  1208.5 33.9 all-gather.1
  1281.5 27.1 reduce-scatter.1
  1317.5 33.9 all-gather.1
  1390.5 27.1 reduce-scatter.1
  1426.3 33.9 all-gather.1
  1499.3 27.1 reduce-scatter.1
  1535.3 33.9 all-gather.1
  1608.3 27.1 reduce-scatter.1
  1644.3 33.9 all-gather.1
  1717.4 27.1 reduce-scatter.1
  1753.1 33.9 all-gather.1
  1826.1 27.1 reduce-scatter.1
  1862.1 33.9 all-gather.1
  1935.2 27.1 reduce-scatter.1
  1970.9 33.9 all-gather.1
  2043.9 27.1 reduce-scatter.1
  2079.7 33.9 all-gather.1
  2152.7 27.1 reduce-scatter.1
  2188.7 33.9 all-gather.1
  2261.7 27.1 reduce-scatter.1
  2297.5 33.9 all-gather.1
  2370.5 27.1 reduce-scatter.1
  2406.3 33.9 all-gather.1
  2479.3 27.1 reduce-scatter.1
where the time goes:
time: 2530 us; the launch traced here: 2520 us
  waiting for transfers between devices  1450 us (57%)
  matrix products  683 us (27%)
  other arithmetic  259 us (10%)
  local copies, waits for them, and re-layouts  77.9 us (3%)
  starting transfers between devices  31.3 us (1%)
    all_gather x23, waiting for transfers between devices, stage_layer(): x_full = lax.all_gather(x_shard, 'tp', axis=1, tiled=True)  779 us
    reduce_scatter x23, waiting for transfers between devices, stage_layer(): lax.psum_scatter(partial_sum, 'tp', scatter_dimension=1, tiled=True)  602 us
    dot_general x23, matrix products, branch_partial(): jnp.dot(hidden, w_down, preferred_element_type=jnp.float32)  394 us
    dot_general x23, matrix products, branch_partial(): jnp.einsum('bktgh,kghd->btd', context, w_o, preferred_element_type=jnp.fl...  121 us
    ppermute x23, waiting for transfers between devices, micro_step(): recv_buf = lax.ppermute(layer_out, 'pp', send_pairs)  67.7 us
    convert_element_type x23, other arithmetic, layer_norm(): (centred * lax.rsqrt(variance + LN_EPS) * ln_gain + ln_bias).astype(jnp.b...  53.9 us
    reduce_sum x23, other arithmetic, layer_norm(): variance = jnp.mean(centred * centred, axis=-1, keepdims=True)  52.5 us
    sub x23, matrix products, causal_attention(): jax.nn.softmax(jnp.where(allowed, scores, -1e+30), axis=-1)  50.6 us
  transfers between devices with their start and end apart: 69, of which 69 were waited for; matrix products, arithmetic and copies ran while one was open for 1% of the time, Pallas kernels for 0%

commit v1 on v0

v1 whole, which is shorter than its diff:
```python
import functools

import jax
import jax.numpy as jnp
import numpy as np
from jax import lax
from jax.experimental import pallas as pl
from jax.experimental.pallas import tpu as pltpu
from jax.sharding import PartitionSpec as P

LN_EPS = 1e-5
ROPE_BASE = 10000.0
F32, BF16 = jnp.float32, jnp.bfloat16
MESH = pl.DeviceIdType.MESH
X_AHEAD = 2


def rope_tables(seq_len, head_dim, heads):
    half = head_dim // 2
    inv_freq = (ROPE_BASE ** (-2.0 * np.arange(half) / head_dim)).astype(np.float32)
    angles = np.arange(seq_len, dtype=np.float32)[:, None] * inv_freq[None, :]
    cos = np.tile(np.cos(angles.astype(np.float64)), (1, heads)).astype(np.float32)
    sin = np.tile(np.sin(angles.astype(np.float64)), (1, heads)).astype(np.float32)
    scale = np.float32(head_dim ** -0.5)
    return np.stack([cos * scale, sin * scale, cos, sin])


def head_masks(head_dim, heads):
    half = head_dim // 2
    lanes = np.arange(heads * head_dim)
    roped = np.stack([(lanes % (heads * half)) // half == head for head in range(heads)])
    plain = np.stack([lanes // head_dim == head for head in range(heads)])
    return np.stack([roped, plain]).astype(np.float32)


def layer_norms(x, ln_ref, h_attn, h_mlp, acc):
    x_f32 = x.astype(F32)
    acc[...] = x_f32
    centred = x_f32 - jnp.mean(x_f32, axis=-1, keepdims=True)
    variance = jnp.mean(centred * centred, axis=-1, keepdims=True)
    normed = centred * lax.rsqrt(variance + LN_EPS)
    h_attn[...] = (normed * ln_ref[0:1, :] + ln_ref[1:2, :]).astype(BF16)
    h_mlp[...] = (normed * ln_ref[2:3, :] + ln_ref[3:4, :]).astype(BF16)


def add_quarter(heads, h_attn, h_mlp, acc, w_qkv, w_up, w_out, rope, masks, mixed):
    seq_len = h_attn.shape[0]
    width = w_qkv.shape[1] // 3
    half = width // 2
    qkv = jnp.dot(h_attn[...], w_qkv[...], preferred_element_type=F32)
    q1, q2 = qkv[:, :half], qkv[:, half:width]
    k1, k2 = qkv[:, width:width + half], qkv[:, width + half:2 * width]
    v = qkv[:, 2 * width:].astype(BF16)
    cos_q, sin_q, cos_k, sin_k = rope[0], rope[1], rope[2], rope[3]
    q = jnp.concatenate([q1 * cos_q - q2 * sin_q, q2 * cos_q + q1 * sin_q], axis=1).astype(BF16)
    k = jnp.concatenate([k1 * cos_k - k2 * sin_k, k2 * cos_k + k1 * sin_k], axis=1).astype(BF16)
    k_heads = jnp.concatenate([k * masks[0, h:h + 1, :] for h in range(heads)], axis=0)
    v_heads = jnp.concatenate([v * masks[1, h:h + 1, :] for h in range(heads)], axis=0)
    scores = lax.dot_general(q, k_heads, (((1,), (1,)), ((), ())), preferred_element_type=F32)
    row = lax.broadcasted_iota(jnp.int32, (seq_len, seq_len), 0)
    col = lax.broadcasted_iota(jnp.int32, (seq_len, seq_len), 1)
    allowed = row >= col
    probs = []
    for h in range(heads):
        masked = jnp.where(allowed, scores[:, h * seq_len:(h + 1) * seq_len], -1e30)
        top = jnp.max(masked, axis=1, keepdims=True)
        weight = jnp.exp(masked - top)
        probs.append((weight * (1.0 / jnp.sum(weight, axis=1, keepdims=True))).astype(BF16))
    context = jnp.dot(jnp.concatenate(probs, axis=1), v_heads, preferred_element_type=F32)
    mixed[:, :width] = context.astype(BF16)
    up = jnp.dot(h_mlp[...], w_up[...], preferred_element_type=F32)
    mixed[:, width:] = ((0.5 * up) * (1.0 + lax.erf(up * np.float32(0.5 ** 0.5)))).astype(BF16)
    acc[...] += jnp.dot(mixed[...], w_out[...], preferred_element_type=F32)


def kernel(tp_size, pp_size, heads, x_hbm, ln_ref, wq_hbm, wk_hbm, wv_hbm, wo_hbm, wup_hbm, wdown_hbm, rope, masks, out_hbm,
           w_qkv, w_up, w_out, raw, xs, ys, h_attn, h_mlp, acc, mixed,
           load_sem, own_send, fwd_send, near_recv, far_recv, x_send, x_recv, x_local,
           pp_send, pp_recv, o_send, o_recv, o_local):
    me = lax.axis_index("tp")
    stage = lax.axis_index("pp")
    right, left = lax.rem(me + 1, tp_size), lax.rem(me + tp_size - 1, tp_size)
    far = lax.rem(me + 2, tp_size)
    nxt = lax.rem(stage + 1, pp_size)
    prv = lax.rem(stage + pp_size - 1, pp_size)
    num_micro, num_seq, seq_len, d_model = xs.shape
    tokens = seq_len // tp_size
    width = raw.shape[1]

    barrier = pltpu.get_barrier_semaphore()
    for step in range(1, tp_size):
        pl.semaphore_signal(barrier, inc=1, device_id={"tp": lax.rem(me + step, tp_size)}, device_id_type=MESH)
    for peer in (nxt, prv):
        pl.semaphore_signal(barrier, inc=1, device_id={"pp": peer}, device_id_type=MESH)

    loads = [
        pltpu.make_async_copy(wo_hbm, w_out.at[me, pl.ds(0, width)], load_sem.at[0]),
        pltpu.make_async_copy(wdown_hbm, w_out.at[me, pl.ds(width, wdown_hbm.shape[0])], load_sem.at[1]),
        pltpu.make_async_copy(wup_hbm, w_up.at[me], load_sem.at[2]),
        pltpu.make_async_copy(wq_hbm, raw.at[0], load_sem.at[3]),
        pltpu.make_async_copy(wk_hbm, raw.at[1], load_sem.at[4]),
        pltpu.make_async_copy(wv_hbm, raw.at[2], load_sem.at[5]),
    ]
    for load in loads:
        load.start()
    pl.semaphore_wait(barrier, tp_size + 1)

    def x_copy(micro, step):
        peer = lax.rem(me + step, tp_size)
        return pltpu.make_async_remote_copy(
            src_ref=x_hbm.at[micro, pl.ds(peer * num_seq, num_seq)],
            dst_ref=xs.at[micro, :, pl.ds(pl.multiple_of(me * tokens, tokens), tokens), :],
            send_sem=x_send.at[micro, step - 1], recv_sem=x_recv.at[micro, step - 1],
            device_id={"tp": peer}, device_id_type=MESH)

    def x_own(micro):
        return pltpu.make_async_copy(
            x_hbm.at[micro, pl.ds(me * num_seq, num_seq)],
            xs.at[micro, :, pl.ds(pl.multiple_of(me * tokens, tokens), tokens), :], x_local.at[micro])

    def send_x(micro):
        x_own(micro).start()
        for step in range(1, tp_size):
            x_copy(micro, step).start()

    @pl.when(stage == 0)
    def _():
        for micro in range(X_AHEAD):
            send_x(micro)

    def halves(ref):
        rows = ref.shape[1] // 2
        return [(ref, 0, rows), (ref, rows, rows)]

    chunks = halves(w_out) + halves(w_up) + halves(w_qkv)

    def shard_copy(index, owner, send_sem, recv_sem, peer):
        ref, start, rows = chunks[index]
        piece = ref.at[owner, pl.ds(start, rows)]
        return pltpu.make_async_remote_copy(
            src_ref=piece, dst_ref=piece, send_sem=send_sem, recv_sem=recv_sem, device_id={"tp": peer}, device_id_type=MESH)

    def own_copy(index, way):
        return shard_copy(index, me, own_send.at[way, index], near_recv.at[way, index], right if way == 0 else left)

    def near_copy(index, way):
        return shard_copy(index, left if way == 0 else right, own_send.at[way, index], near_recv.at[way, index],
                          right if way == 0 else left)

    def fwd_copy(index):
        way = index % 2
        return shard_copy(index, left if way == 0 else right, fwd_send.at[index], far_recv.at[index],
                          right if way == 0 else left)

    def far_copy(index):
        return shard_copy(index, far, fwd_send.at[index], far_recv.at[index], right)

    for load in loads[:2]:
        load.wait()
    for way in range(2):
        own_copy(way, way).start()
    for way in range(2):
        own_copy(1 - way, way).start()
    loads[2].wait()
    for way in range(2):
        own_copy(2 + way, way).start()
    for way in range(2):
        own_copy(3 - way, way).start()
    for load in loads[3:]:
        load.wait()
    head_dim = width // heads
    part = head_dim // 2
    for which in range(3):
        starts = [head * head_dim + side * part for side in range(2) for head in range(heads)]
        if which == 2:
            starts = list(range(0, width, part))
        for col in range(0, d_model, width):
            block = jnp.concatenate([raw[which, start:start + part, col:col + width] for start in starts], axis=0)
            w_qkv[me, col:col + width, which * width:(which + 1) * width] = block.T
    for way in range(2):
        near_copy(way, way).wait_recv()
        fwd_copy(way).start()
    for way in range(2):
        own_copy(4 + way, way).start()
    for way in range(2):
        own_copy(5 - way, way).start()
    for way in range(2):
        near_copy(2 + way, way).wait_recv()
        fwd_copy(2 + way).start()
    for way in range(2):
        near_copy(4 + way, way).wait_recv()
        fwd_copy(4 + way).start()
    for way in range(2):
        for index in range(0, len(chunks), 2):
            near_copy(index + 1 - way, way).wait_recv()
    for index in range(len(chunks)):
        far_copy(index).wait_recv()

    def pp_copy(micro, seq):
        return pltpu.make_async_remote_copy(
            src_ref=ys.at[micro, seq], dst_ref=xs.at[micro, seq], send_sem=pp_send.at[micro, seq],
            recv_sem=pp_recv.at[micro, seq], device_id={"pp": nxt}, device_id_type=MESH)

    def o_copy(micro, step):
        peer = lax.rem(me + step, tp_size)
        return pltpu.make_async_remote_copy(
            src_ref=ys.at[micro, :, pl.ds(pl.multiple_of(peer * tokens, tokens), tokens), :],
            dst_ref=out_hbm.at[micro, pl.ds(me * num_seq, num_seq)],
            send_sem=o_send.at[micro, step - 1], recv_sem=o_recv.at[micro, step - 1],
            device_id={"tp": peer}, device_id_type=MESH)

    def o_own(micro):
        return pltpu.make_async_copy(
            ys.at[micro, :, pl.ds(pl.multiple_of(me * tokens, tokens), tokens), :],
            out_hbm.at[micro, pl.ds(me * num_seq, num_seq)], o_local.at[micro])

    def unit(index, _):
        micro = index // num_seq
        seq = lax.rem(index, num_seq)

        @pl.when((stage == 0) & (seq == 0))
        def _():
            @pl.when(micro + X_AHEAD < num_micro)
            def _():
                send_x(micro + X_AHEAD)
            x_own(micro).wait()
            for step in range(1, tp_size):
                x_copy(micro, step).wait_recv()

        @pl.when(stage > 0)
        def _():
            pp_copy(micro, seq).wait_recv()

        layer_norms(xs[micro, seq], ln_ref, h_attn, h_mlp, acc)
        for shard in range(tp_size):
            add_quarter(heads, h_attn, h_mlp, acc, w_qkv.at[shard], w_up.at[shard], w_out.at[shard], rope, masks, mixed)
        ys[micro, seq] = acc[...].astype(BF16)

        @pl.when(stage < pp_size - 1)
        def _():
            pp_copy(micro, seq).start()

        @pl.when(seq == num_seq - 1)
        def _():
            o_own(micro).start()
            for step in range(1, tp_size):
                o_copy(micro, step).start()
        return 0

    lax.fori_loop(0, num_micro * num_seq, unit, 0)

    for index in range(len(chunks)):
        for way in range(2):
            own_copy(index, way).wait_send()
        fwd_copy(index).wait_send()

    def drain(micro, _):
        @pl.when(stage == 0)
        def _():
            for step in range(1, tp_size):
                x_copy(micro, step).wait_send()

        @pl.when(stage < pp_size - 1)
        def _():
            for seq in range(num_seq):
                pp_copy(micro, seq).wait_send()
        o_own(micro).wait()
        for step in range(1, tp_size):
            o_copy(micro, step).wait_send()
            o_copy(micro, step).wait_recv()
        return 0

    lax.fori_loop(0, num_micro, drain, 0)


def solution(mesh):
    tp_size, pp_size = mesh.shape["tp"], mesh.shape["pp"]

    def stage_body(x_in, ln_params, w_q, w_k, w_v, w_o, w_up, w_down):
        num_micro, batch, tokens, d_model = x_in.shape
        heads, head_dim = w_k.shape[2:]
        width = heads * head_dim
        hidden = w_up.shape[2]
        seq_len = tokens * tp_size
        num_seq = batch // tp_size
        rope = jnp.asarray(rope_tables(seq_len, head_dim, heads))
        masks = jnp.asarray(head_masks(head_dim, heads), dtype=BF16)
        wq_t = jnp.transpose(w_q[0], (1, 2, 3, 0)).reshape(width, d_model)
        wk_t = jnp.transpose(w_k[0], (1, 2, 0)).reshape(width, d_model)
        wv_t = jnp.transpose(w_v[0], (1, 2, 0)).reshape(width, d_model)
        vmem = pl.BlockSpec(memory_space=pltpu.VMEM)
        hbm = pl.BlockSpec(memory_space=pl.ANY)
        dma = pltpu.SemaphoreType.DMA
        others = tp_size - 1
        out = pl.pallas_call(
            functools.partial(kernel, tp_size, pp_size, heads),
            out_shape=jax.ShapeDtypeStruct(x_in.shape, BF16),
            in_specs=[hbm, vmem, hbm, hbm, hbm, hbm, hbm, hbm, vmem, vmem],
            out_specs=hbm,
            scratch_shapes=[
                pltpu.VMEM((tp_size, d_model, 3 * width), BF16),
                pltpu.VMEM((tp_size, d_model, hidden), BF16),
                pltpu.VMEM((tp_size, width + hidden, d_model), BF16),
                pltpu.VMEM((3, width, d_model), BF16),
                pltpu.VMEM((num_micro, num_seq, seq_len, d_model), BF16),
                pltpu.VMEM((num_micro, num_seq, seq_len, d_model), BF16),
                pltpu.VMEM((seq_len, d_model), BF16),
                pltpu.VMEM((seq_len, d_model), BF16),
                pltpu.VMEM((seq_len, d_model), F32),
                pltpu.VMEM((seq_len, width + hidden), BF16),
                dma((6,)), dma((2, 6)), dma((6,)), dma((2, 6)), dma((6,)),
                dma((num_micro, others)), dma((num_micro, others)), dma((num_micro,)),
                dma((num_micro, num_seq)), dma((num_micro, num_seq)),
                dma((num_micro, others)), dma((num_micro, others)), dma((num_micro,)),
            ],
            compiler_params=pltpu.CompilerParams(
                collective_id=0, has_side_effects=True, vmem_limit_bytes=63 * 1024 * 1024),
            name="stage",
        )(x_in, ln_params[0], wq_t, wk_t, wv_t, w_o[0].reshape(width, d_model), w_up[0], w_down[0], rope, masks)
        return out[None]

    in_specs = (P(None, "dp", "tp", None), P("pp", None, None), P("pp", None, "tp", None, None), P("pp", None, "tp", None), P("pp", None, "tp", None), P("pp", "tp", None, None, None), P("pp", None, "tp"), P("pp", "tp", None))
    return jax.shard_map(stage_body, mesh=mesh, in_specs=in_specs, out_specs=P("pp", None, "dp", "tp", None), check_vma=False)
```

time: 2530 us -> 476 us (0.19)
  waiting for transfers between devices: 1450 us -> 0 us
  matrix products: 683 us -> 0 us
  Pallas kernels: 0 us -> 467 us
  other arithmetic: 259 us -> 0 us
  local copies, waits for them, and re-layouts: 77.9 us -> 8.65 us
  starting transfers between devices: 31.3 us -> 0 us
    all_gather x23 -> x0, waiting for transfers between devices: 779 us -> none  [stage_layer(): x_full = lax.all_gather(x_shard, 'tp', axis=1, tiled=True)]
    dot_general x115 -> x0, matrix products: 633 us -> none  [the longest x23 394 us: branch_partial(): jnp.dot(hidden, w_down, preferred_element_type=jnp.float32)]
    reduce_scatter x23 -> x0, waiting for transfers between devices: 602 us -> none  [stage_layer(): lax.psum_scatter(partial_sum, 'tp', scatter_dimension=1, tiled=True)]
    pallas_call x0 -> x1, Pallas kernels: none -> 467 us  [stage_body(): pl.pallas_call(functools.partial(kernel, tp_size, pp_size, heads), out_sh...]
    reduce_sum x46 -> x0, other arithmetic: 100 us -> none  [the longest x23 52.5 us: layer_norm(): variance = jnp.mean(centred * centred, axis=-1, keepdims=True)]
    ppermute x23 -> x0, waiting for transfers between devices: 67.7 us -> none  [micro_step(): recv_buf = lax.ppermute(layer_out, 'pp', send_pairs)]
    convert_element_type x23 -> x0, other arithmetic: 53.9 us -> none  [layer_norm(): (centred * lax.rsqrt(variance + LN_EPS) * ln_gain + ln_bias).astype(jnp.b...]
    sub x23 -> x0, matrix products: 50.6 us -> none  [causal_attention(): jax.nn.softmax(jnp.where(allowed, scores, -1e+30), axis=-1)]
  transfers between devices with their start and end apart: 69 -> 0, of which waited for: 69 -> 0; matrix products, arithmetic and copies ran while one was open for 1% -> 0% of each run, Pallas kernels for 0% -> 0%
where the time goes in v1:
time: 476 us
  Pallas kernels  467 us (98%)
  local copies, waits for them, and re-layouts  8.65 us (2%)
    pallas_call x1, Pallas kernels, stage_body(): pl.pallas_call(functools.partial(kernel, tp_size, pp_size, heads), out_sh...  467 us

profile of v1, /device:TPU:103, one launch (start us, length us, event | category | flops | bytes accessed | tf_op | source)
XLA Modules:
  0.0 476.0 jit_solution(13004950641193147848)
XLA Ops:
  0.0 467.4 %stage.1 = bf16[16,8,32,1024]{3,2,1,0:T(8,128)(2,1)} custom-call(bf16[16,8,32,1024]{3,2,1,0:T(8,128)(2,1)} %x_hbm.1, f32[4,1024]{1,0:T(4,128)} %bitcast.27, bf16[256,1024]{1,0:T(8,128)(2,1)} %bitcast.23, bf16[256,1024]{1,0:T(8,128)(2,1)} %bitcast.24, bf16[256,1024]{1,0:T(8,128)(2,1)} %bitcast.25, bf16[256,1024]{1,0:T(8,128)(2,1)} %bitcast.26, ...), custom_call_target="tpu_custom_call" | custom-call | tf_op jit(solution)/shard_map/stage/pallas_call | solution.py:295
  467.4 8.6 %copy.12 = bf16[1,16,8,32,1024]{4,3,2,1,0:T(8,128)(2,1)} copy(bf16[1,16,8,32,1024]{4,3,2,1,0:T(8,128)(2,1)} %bitcast.20) | data formatting | bytes 16777216

commit v2 on v1

v2 whole, which is shorter than its diff:
```python
import functools

import jax
import jax.numpy as jnp
import numpy as np
from jax import lax
from jax.experimental import pallas as pl
from jax.experimental.pallas import tpu as pltpu
from jax.sharding import PartitionSpec as P

LN_EPS = 1e-5
ROPE_BASE = 10000.0
F32, BF16 = jnp.float32, jnp.bfloat16
MESH = pl.DeviceIdType.MESH


def rope_tables(seq_len, head_dim, heads):
    half = head_dim // 2
    inv_freq = (ROPE_BASE ** (-2.0 * np.arange(half) / head_dim)).astype(np.float32)
    angles = np.arange(seq_len, dtype=np.float32)[:, None] * inv_freq[None, :]
    cos = np.tile(np.cos(angles.astype(np.float64)), (1, heads)).astype(np.float32)
    sin = np.tile(np.sin(angles.astype(np.float64)), (1, heads)).astype(np.float32)
    scale = np.float32(head_dim ** -0.5)
    return np.stack([cos * scale, sin * scale, cos, sin])


def head_masks(head_dim, heads):
    half = head_dim // 2
    lanes = np.arange(heads * head_dim)
    roped = np.stack([(lanes % (heads * half)) // half == head for head in range(heads)])
    plain = np.stack([lanes // head_dim == head for head in range(heads)])
    return np.stack([roped, plain]).astype(np.float32)


def dot(lhs, rhs):
    return jnp.dot(lhs, rhs, preferred_element_type=F32)


def layer_norms(x, ln_ref, h_attn, h_mlp, acc):
    x_f32 = x.astype(F32)
    acc[...] = x_f32
    centred = x_f32 - jnp.mean(x_f32, axis=-1, keepdims=True)
    variance = jnp.mean(centred * centred, axis=-1, keepdims=True)
    normed = centred * lax.rsqrt(variance + LN_EPS)
    h_attn[...] = (normed * ln_ref[0:1, :] + ln_ref[1:2, :]).astype(BF16)
    h_mlp[...] = (normed * ln_ref[2:3, :] + ln_ref[3:4, :]).astype(BF16)


def roped(first, second, cos, sin):
    return jnp.concatenate([first * cos - second * sin, second * cos + first * sin], axis=1).astype(BF16)


def causal_softmax(scores, allowed):
    masked = jnp.where(allowed, scores, -1e30)
    weight = jnp.exp(masked - jnp.max(masked, axis=1, keepdims=True))
    return (weight * (1.0 / jnp.sum(weight, axis=1, keepdims=True))).astype(BF16)


def gelu_of_half(half_x):
    return (half_x * (1.0 + lax.erf(half_x * np.float32(2.0 ** 0.5)))).astype(BF16)


def add_layer(heads, shards, h_attn, h_mlp, acc, w_qkv, w_up, w_out, rope, masks, mixed):
    seq_len, d_model = acc.shape
    width = w_qkv.shape[2] // 3
    half = width // 2
    cols = d_model // heads
    hidden = w_up.shape[2] // heads
    allowed = lax.broadcasted_iota(jnp.int32, (seq_len, seq_len), 0) >= lax.broadcasted_iota(jnp.int32, (seq_len, seq_len), 1)

    def add_out(turn, part):
        piece = pl.ds(part * cols, cols)
        acc[:, piece] += dot(mixed[turn % 2], w_out[shards[turn], :, piece])

    def add_up(turn, part):
        up = dot(h_mlp[...], w_up[shards[turn], :, pl.ds(part * hidden, hidden)])
        mixed[turn % 2, :, pl.ds(width + part * hidden, hidden)] = gelu_of_half(up)

    for turn, shard in enumerate(shards):
        weights = w_qkv.at[shard]
        q = dot(h_attn[...], weights[:, :width])
        k = dot(h_attn[...], weights[:, width:2 * width])
        v = dot(h_attn[...], weights[:, 2 * width:]).astype(BF16)
        q = roped(q[:, :half], q[:, half:], rope[0], rope[1])
        k = roped(k[:, :half], k[:, half:], rope[2], rope[3])
        probs = []
        for head in range(heads):
            if head % 2 == 0:
                k_pair = jnp.concatenate([k * masks[0, h:h + 1, :] for h in (head, head + 1)], axis=0)
                scores = lax.dot_general(q, k_pair, (((1,), (1,)), ((), ())), preferred_element_type=F32)
            if turn == 0:
                add_up(turn, head)
            else:
                add_out(turn - 1, head)
            side = head % 2 * seq_len
            probs.append(causal_softmax(scores[:, side:side + seq_len], allowed))

        def add_context():
            v_heads = jnp.concatenate([v * masks[1, h:h + 1, :] for h in range(heads)], axis=0)
            mixed[turn % 2, :, :width] = dot(jnp.concatenate(probs, axis=1), v_heads).astype(BF16)

        if turn == 0:
            add_context()
        else:
            for part in range(heads):
                add_up(turn, part)
                if part == 1:
                    add_context()
    for part in range(heads):
        add_out(len(shards) - 1, part)


def kernel(tp_size, pp_size, heads, x_hbm, ln_ref, wq_hbm, wk_hbm, wv_hbm, wo_hbm, wup_hbm, wdown_hbm, rope, masks, out,
           w_qkv, w_up, w_out, raw, xs, ys, relay, h_attn, h_mlp, acc, mixed,
           load_sem, own_send, fwd_send, near_recv, far_recv, x_send, x_recv, x_local,
           pp_send, pp_recv, o_send, o_recv, o_local, relay_send, relay_recv):
    me = lax.axis_index("tp")
    stage = lax.axis_index("pp")
    right, left = lax.rem(me + 1, tp_size), lax.rem(me + tp_size - 1, tp_size)
    far = lax.rem(me + 2, tp_size)
    odd = lax.rem(me, 2) == 1
    nxt = lax.rem(stage + 1, pp_size)
    prv = lax.rem(stage + pp_size - 1, pp_size)
    last_stage = pp_size - 1
    num_micro, num_seq, seq_len, d_model = xs.shape
    tokens = seq_len // tp_size
    width = raw.shape[1]

    barrier = pltpu.get_barrier_semaphore()
    for step in range(1, tp_size):
        pl.semaphore_signal(barrier, inc=1, device_id={"tp": lax.rem(me + step, tp_size)}, device_id_type=MESH)
    for peer in (nxt, prv):
        pl.semaphore_signal(barrier, inc=1, device_id={"pp": peer}, device_id_type=MESH)

    loads = [
        pltpu.make_async_copy(wo_hbm, w_out.at[me, pl.ds(0, width)], load_sem.at[0]),
        pltpu.make_async_copy(wdown_hbm, w_out.at[me, pl.ds(width, wdown_hbm.shape[0])], load_sem.at[1]),
        pltpu.make_async_copy(wup_hbm, w_up.at[me], load_sem.at[2]),
        pltpu.make_async_copy(wq_hbm, raw.at[0], load_sem.at[3]),
        pltpu.make_async_copy(wk_hbm, raw.at[1], load_sem.at[4]),
        pltpu.make_async_copy(wv_hbm, raw.at[2], load_sem.at[5]),
    ]
    for load in loads:
        load.start()
    pl.semaphore_wait(barrier, tp_size + 1)

    def token_rows(owner):
        return pl.ds(pl.multiple_of(owner * tokens, tokens), tokens)

    def seq_rows(owner):
        return pl.ds(owner * num_seq, num_seq)

    def x_copy(micro, step):
        peer = lax.rem(me + step, tp_size)
        return pltpu.make_async_remote_copy(
            src_ref=x_hbm.at[micro, seq_rows(peer)], dst_ref=ys.at[micro, :, token_rows(me), :],
            send_sem=x_send.at[micro, step - 1], recv_sem=x_recv.at[micro, step - 1],
            device_id={"tp": peer}, device_id_type=MESH)

    def x_own(micro):
        return pltpu.make_async_copy(
            x_hbm.at[micro, seq_rows(me)], ys.at[micro, :, token_rows(me), :], x_local.at[micro])

    def pp_copy(micro, seq):
        return pltpu.make_async_remote_copy(
            src_ref=ys.at[micro, seq], dst_ref=xs.at[micro, seq], send_sem=pp_send.at[micro, seq],
            recv_sem=pp_recv.at[micro, seq], device_id={"pp": nxt}, device_id_type=MESH)

    @pl.when(stage == last_stage)
    def _():
        def collect(micro, _):
            x_own(micro).start()
            for step in range(1, tp_size):
                x_copy(micro, step).start()
            return 0
        lax.fori_loop(0, num_micro, collect, 0)

    def halves(ref):
        rows = ref.shape[1] // 2
        return [(ref, 0, rows), (ref, rows, rows)]

    chunks = halves(w_out) + halves(w_up) + halves(w_qkv)

    def shard_copy(index, owner, send_sem, recv_sem, peer):
        ref, start, rows = chunks[index]
        piece = ref.at[owner, pl.ds(start, rows)]
        return pltpu.make_async_remote_copy(
            src_ref=piece, dst_ref=piece, send_sem=send_sem, recv_sem=recv_sem, device_id={"tp": peer}, device_id_type=MESH)

    def own_copy(index, way):
        return shard_copy(index, me, own_send.at[way, index], near_recv.at[way, index], right if way == 0 else left)

    def near_copy(index, way):
        return shard_copy(index, left if way == 0 else right, own_send.at[way, index], near_recv.at[way, index],
                          right if way == 0 else left)

    def fwd_copy(index):
        way = index % 2
        return shard_copy(index, left if way == 0 else right, fwd_send.at[index], far_recv.at[index],
                          right if way == 0 else left)

    def far_copy(index):
        return shard_copy(index, far, fwd_send.at[index], far_recv.at[index], right)

    def send_own(first):
        for way in range(2):
            own_copy(first + way, way).start()
        for way in range(2):
            own_copy(first + 1 - way, way).start()

    for load in loads[:2]:
        load.wait()
    send_own(0)
    loads[2].wait()
    send_own(2)
    for load in loads[3:]:
        load.wait()
    head_dim = width // heads
    part = head_dim // 2
    for which in range(3):
        starts = [head * head_dim + side * part for side in range(2) for head in range(heads)]
        if which == 2:
            starts = list(range(0, width, part))
        for col in range(0, d_model, width):
            block = jnp.concatenate([raw[which, start:start + part, col:col + width] for start in starts], axis=0)
            w_qkv[me, col:col + width, which * width:(which + 1) * width] = block.T

    @pl.when(stage == last_stage)
    def _():
        def hand_on(micro, _):
            x_own(micro).wait()
            for step in range(1, tp_size):
                x_copy(micro, step).wait_recv()
            for seq in range(num_seq):
                pp_copy(micro, seq).start()
            return 0
        lax.fori_loop(0, num_micro, hand_on, 0)

    for way in range(2):
        near_copy(way, way).wait_recv()
        fwd_copy(way).start()
    send_own(4)
    for first in (2, 4):
        for way in range(2):
            near_copy(first + way, way).wait_recv()
            fwd_copy(first + way).start()
    for way in range(2):
        for index in range(0, len(chunks), 2):
            near_copy(index + 1 - way, way).wait_recv()
    for index in range(len(chunks)):
        far_copy(index).wait_recv()

    @pl.when(stage == last_stage)
    def _():
        def handed(micro, _):
            for seq in range(num_seq):
                pp_copy(micro, seq).wait_send()
            return 0
        lax.fori_loop(0, num_micro, handed, 0)

    def o_copy(micro, step):
        peer = lax.rem(me + step, tp_size)
        return pltpu.make_async_remote_copy(
            src_ref=ys.at[micro, :, token_rows(peer), :], dst_ref=out.at[micro, seq_rows(me)],
            send_sem=o_send.at[micro, step - 1], recv_sem=o_recv.at[micro, step - 1],
            device_id={"tp": peer}, device_id_type=MESH)

    def o_own(micro):
        return pltpu.make_async_copy(ys.at[micro, :, token_rows(me), :], out.at[micro, seq_rows(me)], o_local.at[micro])

    def relay_copy(micro):
        return pltpu.make_async_remote_copy(
            src_ref=ys.at[micro, :, token_rows(far), :], dst_ref=relay.at[micro],
            send_sem=o_send.at[micro, 1], recv_sem=relay_recv.at[micro],
            device_id={"tp": jnp.where(odd, left, right)}, device_id_type=MESH)

    def pass_on(micro):
        return pltpu.make_async_remote_copy(
            src_ref=relay.at[micro], dst_ref=out.at[micro, seq_rows(jnp.where(odd, left, right))],
            send_sem=relay_send.at[micro], recv_sem=o_recv.at[micro, 1],
            device_id={"tp": jnp.where(odd, right, left)}, device_id_type=MESH)

    def unit(index, _):
        micro = index // num_seq
        seq = lax.rem(index, num_seq)
        pp_copy(micro, seq).wait_recv()
        layer_norms(xs[micro, seq], ln_ref, h_attn, h_mlp, acc)
        add_layer(heads, list(range(tp_size)), h_attn, h_mlp, acc, w_qkv, w_up, w_out, rope, masks, mixed)
        ys[micro, seq] = acc[...].astype(BF16)

        @pl.when(stage < last_stage)
        def _():
            pp_copy(micro, seq).start()

        @pl.when((seq == 0) & (micro > 0))
        def _():
            relay_copy(micro - 1).wait_recv()
            pass_on(micro - 1).start()

        @pl.when(seq == num_seq - 1)
        def _():
            o_copy(micro, 1).start()
            o_copy(micro, 3).start()

            @pl.when(micro < num_micro - 1)
            def _():
                relay_copy(micro).start()

            @pl.when(micro == num_micro - 1)
            def _():
                o_copy(micro, 2).start()
            o_own(micro).start()
        return 0

    lax.fori_loop(0, num_micro * num_seq, unit, 0)

    for index in range(len(chunks)):
        for way in range(2):
            own_copy(index, way).wait_send()
        fwd_copy(index).wait_send()

    def drain(micro, _):
        @pl.when(stage == last_stage)
        def _():
            for step in range(1, tp_size):
                x_copy(micro, step).wait_send()

        @pl.when(stage < last_stage)
        def _():
            for seq in range(num_seq):
                pp_copy(micro, seq).wait_send()

        @pl.when(micro < num_micro - 1)
        def _():
            pass_on(micro).wait_send()
        o_own(micro).wait()
        for step in range(1, tp_size):
            o_copy(micro, step).wait_send()
            o_copy(micro, step).wait_recv()
        return 0

    lax.fori_loop(0, num_micro, drain, 0)


def solution(mesh):
    tp_size, pp_size = mesh.shape["tp"], mesh.shape["pp"]

    def stage_body(x_in, ln_params, w_q, w_k, w_v, w_o, w_up, w_down):
        num_micro, batch, tokens, d_model = x_in.shape
        heads, head_dim = w_k.shape[2:]
        width = heads * head_dim
        hidden = w_up.shape[2]
        seq_len = tokens * tp_size
        num_seq = batch // tp_size
        rope = jnp.asarray(rope_tables(seq_len, head_dim, heads))
        masks = jnp.asarray(head_masks(head_dim, heads), dtype=BF16)
        wq_t = jnp.transpose(w_q[0], (1, 2, 3, 0)).reshape(width, d_model)
        wk_t = jnp.transpose(w_k[0], (1, 2, 0)).reshape(width, d_model)
        wv_t = jnp.transpose(w_v[0], (1, 2, 0)).reshape(width, d_model)
        ln_scale = jnp.asarray(np.array([[1.0], [1.0], [0.5], [0.5]], np.float32))
        vmem = pl.BlockSpec(memory_space=pltpu.VMEM)
        hbm = pl.BlockSpec(memory_space=pl.ANY)
        dma = pltpu.SemaphoreType.DMA
        others = tp_size - 1
        out = pl.pallas_call(
            functools.partial(kernel, tp_size, pp_size, heads),
            out_shape=jax.ShapeDtypeStruct(x_in.shape, BF16),
            in_specs=[hbm, vmem, hbm, hbm, hbm, hbm, hbm, hbm, vmem, vmem],
            out_specs=hbm,
            scratch_shapes=[
                pltpu.VMEM((tp_size, d_model, 3 * width), BF16),
                pltpu.VMEM((tp_size, d_model, hidden), BF16),
                pltpu.VMEM((tp_size, width + hidden, d_model), BF16),
                pltpu.VMEM((3, width, d_model), BF16),
                pltpu.VMEM((num_micro, num_seq, seq_len, d_model), BF16),
                pltpu.VMEM((num_micro, num_seq, seq_len, d_model), BF16),
                pltpu.VMEM((num_micro, num_seq, tokens, d_model), BF16),
                pltpu.VMEM((seq_len, d_model), BF16),
                pltpu.VMEM((seq_len, d_model), BF16),
                pltpu.VMEM((seq_len, d_model), F32),
                pltpu.VMEM((2, seq_len, width + hidden), BF16),
                dma((6,)), dma((2, 6)), dma((6,)), dma((2, 6)), dma((6,)),
                dma((num_micro, others)), dma((num_micro, others)), dma((num_micro,)),
                dma((num_micro, num_seq)), dma((num_micro, num_seq)),
                dma((num_micro, others)), dma((num_micro, others)), dma((num_micro,)),
                dma((num_micro,)), dma((num_micro,)),
            ],
            compiler_params=pltpu.CompilerParams(
                collective_id=0, has_side_effects=True, vmem_limit_bytes=63 * 1024 * 1024),
            name="stage",
        )(x_in, ln_params[0] * ln_scale, wq_t, wk_t, wv_t, w_o[0].reshape(width, d_model), w_up[0], w_down[0], rope, masks)
        return out[None]

    in_specs = (P(None, "dp", "tp", None), P("pp", None, None), P("pp", None, "tp", None, None), P("pp", None, "tp", None), P("pp", None, "tp", None), P("pp", "tp", None, None, None), P("pp", None, "tp"), P("pp", "tp", None))
    return jax.shard_map(stage_body, mesh=mesh, in_specs=in_specs, out_specs=P("pp", None, "dp", "tp", None), check_vma=False)
```

time: 476 us -> 438 us (0.920)
  Pallas kernels: 467 us -> 428 us
    pallas_call x1, Pallas kernels: 467 us -> 428 us  [stage_body(): pl.pallas_call(functools.partial(kernel, tp_size, pp_size, heads), out_sh...]
where the time goes in v2:
time: 438 us
  Pallas kernels  428 us (98%)
  local copies, waits for them, and re-layouts  8.65 us (2%)
    pallas_call x1, Pallas kernels, stage_body(): pl.pallas_call(functools.partial(kernel, tp_size, pp_size, heads), out_sh...  428 us

profile of v2, /device:TPU:103, one launch (start us, length us, event | category | flops | bytes accessed | tf_op | source)
XLA Modules:
  0.0 437.9 jit_solution(3710835542046194835)
XLA Ops:
  0.0 1.4 bitcast_multiply_fusion.ln_ref
  1.4 427.8 %stage.1 = bf16[16,8,32,1024]{3,2,1,0:T(8,128)(2,1)} custom-call(bf16[16,8,32,1024]{3,2,1,0:T(8,128)(2,1)} %x_hbm.1, f32[4,1024]{1,0:T(4,128)} %bitcast_multiply_fusion.ln_ref, bf16[256,1024]{1,0:T(8,128)(2,1)} %bitcast.24, bf16[256,1024]{1,0:T(8,128)(2,1)} %bitcast.25, bf16[256,1024]{1,0:T(8,128)(2,1)} %bitcast.26, bf16[256,1024]{1,0:T(8,128)(2,1)} %bitcast.27, ...), custom_call_target="tpu_custom_call" | custom-call | tf_op jit(solution)/shard_map/stage/pallas_call | solution.py:365
  429.2 8.6 %copy.13 = bf16[1,16,8,32,1024]{4,3,2,1,0:T(8,128)(2,1)} copy(bf16[1,16,8,32,1024]{4,3,2,1,0:T(8,128)(2,1)} %bitcast.21) | data formatting | bytes 16777216

commit v3 on v2

--- a/solution.py
+++ b/solution.py
@@ -111,14 +111,12 @@
 
 
 def kernel(tp_size, pp_size, heads, x_hbm, ln_ref, wq_hbm, wk_hbm, wv_hbm, wo_hbm, wup_hbm, wdown_hbm, rope, masks, out,
-           w_qkv, w_up, w_out, raw, xs, ys, relay, h_attn, h_mlp, acc, mixed,
-           load_sem, own_send, fwd_send, near_recv, far_recv, x_send, x_recv, x_local,
-           pp_send, pp_recv, o_send, o_recv, o_local, relay_send, relay_recv):
+           w_qkv, w_up, w_out, raw, xs, ys, ln_half, h_attn, h_mlp, acc, mixed,
+           load_sem, w_send, near_recv, far_recv, x_send, x_recv, x_local, pp_send, pp_recv, o_send, o_recv):
     me = lax.axis_index("tp")
     stage = lax.axis_index("pp")
     right, left = lax.rem(me + 1, tp_size), lax.rem(me + tp_size - 1, tp_size)
     far = lax.rem(me + 2, tp_size)
-    odd = lax.rem(me, 2) == 1
     nxt = lax.rem(stage + 1, pp_size)
     prv = lax.rem(stage + pp_size - 1, pp_size)
     last_stage = pp_size - 1
@@ -142,6 +140,8 @@
     ]
     for load in loads:
         load.start()
+    ln_half[...] = ln_ref[...]
+    ln_half[2:4, :] = 0.5 * ln_ref[2:4, :]
     pl.semaphore_wait(barrier, tp_size + 1)
 
     def token_rows(owner):
@@ -154,16 +154,16 @@
         peer = lax.rem(me + step, tp_size)
         return pltpu.make_async_remote_copy(
             src_ref=x_hbm.at[micro, seq_rows(peer)], dst_ref=ys.at[micro, :, token_rows(me), :],
-            send_sem=x_send.at[micro, step - 1], recv_sem=x_recv.at[micro, step - 1],
+            send_sem=x_send, recv_sem=x_recv,
             device_id={"tp": peer}, device_id_type=MESH)
 
     def x_own(micro):
         return pltpu.make_async_copy(
-            x_hbm.at[micro, seq_rows(me)], ys.at[micro, :, token_rows(me), :], x_local.at[micro])
+            x_hbm.at[micro, seq_rows(me)], ys.at[micro, :, token_rows(me), :], x_local)
 
     def pp_copy(micro, seq):
         return pltpu.make_async_remote_copy(
-            src_ref=ys.at[micro, seq], dst_ref=xs.at[micro, seq], send_sem=pp_send.at[micro, seq],
+            src_ref=ys.at[micro, seq], dst_ref=xs.at[micro, seq], send_sem=pp_send,
             recv_sem=pp_recv.at[micro, seq], device_id={"pp": nxt}, device_id_type=MESH)
 
     @pl.when(stage == last_stage)
@@ -188,19 +188,20 @@
             src_ref=piece, dst_ref=piece, send_sem=send_sem, recv_sem=recv_sem, device_id={"tp": peer}, device_id_type=MESH)
 
     def own_copy(index, way):
-        return shard_copy(index, me, own_send.at[way, index], near_recv.at[way, index], right if way == 0 else left)
+        return shard_copy(index, me, w_send, near_recv.at[way, index], right if way == 0 else left)
 
     def near_copy(index, way):
-        return shard_copy(index, left if way == 0 else right, own_send.at[way, index], near_recv.at[way, index],
+        return shard_copy(index, left if way == 0 else right, w_send, near_recv.at[way, index],
                           right if way == 0 else left)
 
     def fwd_copy(index):
         way = index % 2
-        return shard_copy(index, left if way == 0 else right, fwd_send.at[index], far_recv.at[index],
+        return shard_copy(index, left if way == 0 else right, w_send, far_recv.at[index // 2],
                           right if way == 0 else left)
 
-    def far_copy(index):
-        return shard_copy(index, far, fwd_send.at[index], far_recv.at[index], right)
+    def take(sem, *refs):
+        for ref in refs:
+            pltpu.make_async_copy(ref, ref, sem).wait()
 
     def send_own(first):
         for way in range(2):
@@ -225,12 +226,14 @@
             block = jnp.concatenate([raw[which, start:start + part, col:col + width] for start in starts], axis=0)
             w_qkv[me, col:col + width, which * width:(which + 1) * width] = block.T
 
+    others = ys.at[pl.ds(0, num_micro // tp_size * (tp_size - 1))]
+
     @pl.when(stage == last_stage)
     def _():
+        take(x_local, ys.at[pl.ds(0, num_micro // tp_size)])
+        take(x_recv, others)
+
         def hand_on(micro, _):
-            x_own(micro).wait()
-            for step in range(1, tp_size):
-                x_copy(micro, step).wait_recv()
             for seq in range(num_seq):
                 pp_copy(micro, seq).start()
             return 0
@@ -247,44 +250,24 @@
     for way in range(2):
         for index in range(0, len(chunks), 2):
             near_copy(index + 1 - way, way).wait_recv()
-    for index in range(len(chunks)):
-        far_copy(index).wait_recv()
+    for index, ref in enumerate((w_out, w_up, w_qkv)):
+        take(far_recv.at[index], ref.at[far])
 
     @pl.when(stage == last_stage)
     def _():
-        def handed(micro, _):
-            for seq in range(num_seq):
-                pp_copy(micro, seq).wait_send()
-            return 0
-        lax.fori_loop(0, num_micro, handed, 0)
+        take(pp_send, ys)
 
     def o_copy(micro, step):
         peer = lax.rem(me + step, tp_size)
         return pltpu.make_async_remote_copy(
             src_ref=ys.at[micro, :, token_rows(peer), :], dst_ref=out.at[micro, seq_rows(me)],
-            send_sem=o_send.at[micro, step - 1], recv_sem=o_recv.at[micro, step - 1],
-            device_id={"tp": peer}, device_id_type=MESH)
-
-    def o_own(micro):
-        return pltpu.make_async_copy(ys.at[micro, :, token_rows(me), :], out.at[micro, seq_rows(me)], o_local.at[micro])
-
-    def relay_copy(micro):
-        return pltpu.make_async_remote_copy(
-            src_ref=ys.at[micro, :, token_rows(far), :], dst_ref=relay.at[micro],
-            send_sem=o_send.at[micro, 1], recv_sem=relay_recv.at[micro],
-            device_id={"tp": jnp.where(odd, left, right)}, device_id_type=MESH)
-
-    def pass_on(micro):
-        return pltpu.make_async_remote_copy(
-            src_ref=relay.at[micro], dst_ref=out.at[micro, seq_rows(jnp.where(odd, left, right))],
-            send_sem=relay_send.at[micro], recv_sem=o_recv.at[micro, 1],
-            device_id={"tp": jnp.where(odd, right, left)}, device_id_type=MESH)
+            send_sem=o_send, recv_sem=o_recv, device_id={"tp": peer}, device_id_type=MESH)
 
     def unit(index, _):
         micro = index // num_seq
         seq = lax.rem(index, num_seq)
         pp_copy(micro, seq).wait_recv()
-        layer_norms(xs[micro, seq], ln_ref, h_attn, h_mlp, acc)
+        layer_norms(xs[micro, seq], ln_half, h_attn, h_mlp, acc)
         add_layer(heads, list(range(tp_size)), h_attn, h_mlp, acc, w_qkv, w_up, w_out, rope, masks, mixed)
         ys[micro, seq] = acc[...].astype(BF16)
 
@@ -292,54 +275,27 @@
         def _():
             pp_copy(micro, seq).start()
 
-        @pl.when((seq == 0) & (micro > 0))
-        def _():
-            relay_copy(micro - 1).wait_recv()
-            pass_on(micro - 1).start()
+        out[micro, me * num_seq + seq] = ys[micro, seq, token_rows(me), :]
 
         @pl.when(seq == num_seq - 1)
         def _():
-            o_copy(micro, 1).start()
-            o_copy(micro, 3).start()
-
-            @pl.when(micro < num_micro - 1)
-            def _():
-                relay_copy(micro).start()
-
-            @pl.when(micro == num_micro - 1)
-            def _():
-                o_copy(micro, 2).start()
-            o_own(micro).start()
+            for step in range(1, tp_size):
+                o_copy(micro, step).start()
         return 0
 
     lax.fori_loop(0, num_micro * num_seq, unit, 0)
 
-    for index in range(len(chunks)):
-        for way in range(2):
-            own_copy(index, way).wait_send()
-        fwd_copy(index).wait_send()
-
-    def drain(micro, _):
-        @pl.when(stage == last_stage)
-        def _():
-            for step in range(1, tp_size):
-                x_copy(micro, step).wait_send()
-
-        @pl.when(stage < last_stage)
-        def _():
-            for seq in range(num_seq):
-                pp_copy(micro, seq).wait_send()
-
-        @pl.when(micro < num_micro - 1)
-        def _():
-            pass_on(micro).wait_send()
-        o_own(micro).wait()
-        for step in range(1, tp_size):
-            o_copy(micro, step).wait_send()
-            o_copy(micro, step).wait_recv()
-        return 0
-
-    lax.fori_loop(0, num_micro, drain, 0)
+    take(w_send, w_out, w_up)
+
+    @pl.when(stage == last_stage)
+    def _():
+        take(x_send, others)
+
+    @pl.when(stage < last_stage)
+    def _():
+        take(pp_send, ys)
+    take(o_send, others)
+    take(o_recv, others)
 
 
 def solution(mesh):
@@ -357,16 +313,14 @@
         wq_t = jnp.transpose(w_q[0], (1, 2, 3, 0)).reshape(width, d_model)
         wk_t = jnp.transpose(w_k[0], (1, 2, 0)).reshape(width, d_model)
         wv_t = jnp.transpose(w_v[0], (1, 2, 0)).reshape(width, d_model)
-        ln_scale = jnp.asarray(np.array([[1.0], [1.0], [0.5], [0.5]], np.float32))
         vmem = pl.BlockSpec(memory_space=pltpu.VMEM)
         hbm = pl.BlockSpec(memory_space=pl.ANY)
         dma = pltpu.SemaphoreType.DMA
-        others = tp_size - 1
         out = pl.pallas_call(
             functools.partial(kernel, tp_size, pp_size, heads),
-            out_shape=jax.ShapeDtypeStruct(x_in.shape, BF16),
+            out_shape=pltpu.VMEM(x_in.shape, BF16),
             in_specs=[hbm, vmem, hbm, hbm, hbm, hbm, hbm, hbm, vmem, vmem],
-            out_specs=hbm,
+            out_specs=vmem,
             scratch_shapes=[
                 pltpu.VMEM((tp_size, d_model, 3 * width), BF16),
                 pltpu.VMEM((tp_size, d_model, hidden), BF16),
@@ -374,21 +328,17 @@
                 pltpu.VMEM((3, width, d_model), BF16),
                 pltpu.VMEM((num_micro, num_seq, seq_len, d_model), BF16),
                 pltpu.VMEM((num_micro, num_seq, seq_len, d_model), BF16),
-                pltpu.VMEM((num_micro, num_seq, tokens, d_model), BF16),
+                pltpu.VMEM((4, d_model), F32),
                 pltpu.VMEM((seq_len, d_model), BF16),
                 pltpu.VMEM((seq_len, d_model), BF16),
                 pltpu.VMEM((seq_len, d_model), F32),
                 pltpu.VMEM((2, seq_len, width + hidden), BF16),
-                dma((6,)), dma((2, 6)), dma((6,)), dma((2, 6)), dma((6,)),
-                dma((num_micro, others)), dma((num_micro, others)), dma((num_micro,)),
-                dma((num_micro, num_seq)), dma((num_micro, num_seq)),
-                dma((num_micro, others)), dma((num_micro, others)), dma((num_micro,)),
-                dma((num_micro,)), dma((num_micro,)),
+                dma((6,)), dma, dma((2, 6)), dma((3,)), dma, dma, dma, dma, dma((num_micro, num_seq)), dma, dma,
             ],
             compiler_params=pltpu.CompilerParams(
-                collective_id=0, has_side_effects=True, vmem_limit_bytes=63 * 1024 * 1024),
+                collective_id=0, has_side_effects=True, vmem_limit_bytes=54 * 1024 * 1024),
             name="stage",
-        )(x_in, ln_params[0] * ln_scale, wq_t, wk_t, wv_t, w_o[0].reshape(width, d_model), w_up[0], w_down[0], rope, masks)
+        )(x_in, ln_params[0], wq_t, wk_t, wv_t, w_o[0].reshape(width, d_model), w_up[0], w_down[0], rope, masks)
         return out[None]
 
     in_specs = (P(None, "dp", "tp", None), P("pp", None, None), P("pp", None, "tp", None, None), P("pp", None, "tp", None), P("pp", None, "tp", None), P("pp", "tp", None, None, None), P("pp", None, "tp"), P("pp", "tp", None))

time: 438 us -> 418 us (0.954)
  Pallas kernels: 428 us -> 414 us
  local copies, waits for them, and re-layouts: 8.65 us -> 3.4 us
    pallas_call x1, Pallas kernels: 428 us -> 414 us  [stage_body(): pl.pallas_call(functools.partial(kernel, tp_size, pp_size, heads), out_sh...]
    unnamed x1, local copies, waits for them, and re-layouts: 8.65 us -> 3.4 us
where the time goes in v3:
time: 418 us
  Pallas kernels  414 us (99%)
    pallas_call x1, Pallas kernels, stage_body(): pl.pallas_call(functools.partial(kernel, tp_size, pp_size, heads), out_sh...  414 us

profile of v3, /device:TPU:103, one launch (start us, length us, event | category | flops | bytes accessed | tf_op | source)
XLA Modules:
  0.0 417.6 jit_solution(5076603674045761543)
XLA Ops:
  0.0 414.2 %stage.1 = bf16[16,8,32,1024]{3,2,1,0:T(8,128)(2,1)S(1)} custom-call(bf16[16,8,32,1024]{3,2,1,0:T(8,128)(2,1)} %x_hbm.1, f32[4,1024]{1,0:T(4,128)} %bitcast.27, bf16[256,1024]{1,0:T(8,128)(2,1)} %bitcast.23, bf16[256,1024]{1,0:T(8,128)(2,1)} %bitcast.24, bf16[256,1024]{1,0:T(8,128)(2,1)} %bitcast.25, bf16[256,1024]{1,0:T(8,128)(2,1)} %bitcast.26, ...), custom_call_target="tpu_custom_call" | custom-call | tf_op jit(solution)/shard_map/stage/pallas_call | solution.py:319
  414.2 3.4 copy.12
